TPU v7x, 32 devices: a whole 2x2x4 slice. The times are simulated.
32 devices in a mesh: section: 2 (over y), gx: 4 (over z), gy: 4 (over x, core).
Axes of the slice: x: 2, y: 2, z: 4, core: 2. Of those that a mesh axis runs over, the one named last changes fastest.
Arguments:
- load_index: int32 [2], P('section'), may hold values from 0 to 63
- load_table: float32 [64, 3], replicated, may hold values from -4 to 4
- toughness: float32 [2, 64, 64, 128], P('section', 'gx', 'gy'), may hold values from 0.3 to 3
- clamp_mask: int32 [64, 64, 128], P('gx', 'gy'), may hold values 0 or 1
- load_mask: int32 [64, 64, 128], P('gx', 'gy'), may hold values 0 or 1
- crack_mask: int32 [64, 64, 128], P('gx', 'gy'), may hold values 0 or 1
Outputs:
- displacement: float32 [2, 3, 64, 64, 128], P('section', None, 'gx', 'gy')
- damage: float32 [2, 64, 64, 128], P('section', 'gx', 'gy')
- section_residuals: float32 [2, 2], P('section')
All inputs are finite; a program needn't handle non-finite values. No bound on the sum of `clamp_mask` or of `load_mask` or of `crack_mask` on one device may be relied on, other than what follows from the above.
Results may differ from a plain program's by a relative error of at most 0.0003.
Values sent between devices are 32-bit elements; how exact they have to be, the bound alone decides.
A program may use at most 64 MiB of HBM per device.

v0:
```python
import functools
import math

import jax
import jax.numpy as jnp
from jax import lax
from jax.experimental import pallas as pl
from jax.experimental.pallas import tpu as pltpu
from jax.sharding import PartitionSpec as P

relax_weight = 0.6
stiff_floor = 0.001
eigen_guard = 1e-08
MESH = pl.DeviceIdType.MESH

HX = 3
OY = 8

ACOS = (
    1.5707963050,
    -0.2145988016,
    0.0889789874,
    -0.0501743046,
    0.0308918810,
    -0.0170881256,
    0.0066700901,
    -0.0012624911,
)


def up8(n):
    return -(-n // 8) * 8


def spectral_energy(xx, yy, zz, xy, xz, yz):
    trace = xx + yy + zz
    mid = trace * (1.0 / 3.0)
    dx = xx - mid
    dy = yy - mid
    dz = zz - mid
    xy2 = xy * xy
    xz2 = xz * xz
    yz2 = yz * yz
    sixth = (dx * dx + dy * dy + dz * dz + 2.0 * (xy2 + xz2 + yz2)) * (1.0 / 6.0)
    twice_radius = 2.0 * jnp.sqrt(sixth)
    guarded = sixth + eigen_guard
    det = dx * (dy * dz - yz2) - dz * xy2 - dy * xz2 + 2.0 * (xy * xz * yz)
    ratio = det / (2.0 * guarded * jnp.sqrt(guarded))
    size = jnp.minimum(jnp.abs(ratio), 1.0)
    poly = jnp.full_like(size, ACOS[-1] / 3.0)
    for c in ACOS[-2::-1]:
        poly = poly * size + c / 3.0
    t = jnp.sqrt(1.0 - size) * poly
    t2 = t * t
    cos_t = 1.0 + t2 * (-0.5 + t2 * (1.0 / 24.0 + t2 * (-1.0 / 720.0 + t2 * (1.0 / 40320.0))))
    sin_t = t * (1.0 + t2 * (-1.0 / 6.0 + t2 * (1.0 / 120.0 + t2 * (-1.0 / 5040.0))))
    other = 0.5 * cos_t + math.sqrt(0.75) * sin_t
    upper = ratio >= 0.0
    first = jnp.where(upper, cos_t, other)
    last = jnp.where(upper, other, cos_t)
    largest = mid + twice_radius * first
    smallest = mid - twice_radius * last
    between = trace - largest - smallest
    relu = lambda v: jnp.maximum(v, 0.0)
    return (
        0.5 * jnp.square(relu(trace))
        + jnp.square(relu(largest))
        + jnp.square(relu(between))
        + jnp.square(relu(smallest))
    )


def kernel(
    sizes,
    index_hbm,
    table_hbm,
    tough_hbm,
    clamp_hbm,
    load_hbm,
    crack_hbm,
    first_ref,
    second_ref,
    third_ref,
    dam_ref,
    norm_ref,
    index_ref,
    table_ref,
    tough_ref,
    clamp_ref,
    load_ref,
    crack_ref,
    local,
    state,
    stiff,
    flow,
    held,
    pinned,
    free,
    tough_in,
    pack_mask,
    pack_u,
    pack_d,
    in_mask_x,
    in_mask_y,
    in_mask_c,
    in_u_x,
    in_u_x3,
    in_u_y,
    in_u_c,
    in_d_x,
    in_d_y,
    in_d_c,
    sums,
    mask_send,
    mask_recv,
    u_send,
    u_recv,
    d_send,
    d_recv,
    tough_send,
    tough_recv,
    sum_send,
    sum_recv,
):
    sections, ngx, ngy, nx, ny, nz = sizes
    disp_refs = (first_ref, second_ref, third_ref)
    sec = lax.axis_index("section")
    gx = lax.axis_index("gx")
    gy = lax.axis_index("gy")
    group = ngx * ngy
    me = gx * ngy + gy
    peers = []
    for k in range(1, group):
        other = lax.rem(me + k, group)
        peers.append({"gx": other // ngy, "gy": lax.rem(other, ngy)})

    fetch = [
        pltpu.make_async_copy(src, dst, local.at[n])
        for n, (src, dst) in enumerate(
            (
                (load_hbm, load_ref),
                (crack_hbm, crack_ref),
                (clamp_hbm, clamp_ref),
                (tough_hbm, tough_ref),
                (index_hbm, index_ref),
                (table_hbm, table_ref),
            )
        )
    ]
    for copy in fetch:
        copy.start()

    barrier = pltpu.get_barrier_semaphore()
    for peer in peers:
        pl.semaphore_signal(barrier, inc=1, device_id=peer, device_id_type=MESH)
    for k in range(1, sections):
        pl.semaphore_signal(
            barrier,
            inc=1,
            device_id={"section": lax.rem(sec + k, sections)},
            device_id_type=MESH,
        )

    there = {
        "gx": (gx > 0, gx < ngx - 1),
        "gy": (gy > 0, gy < ngy - 1),
    }
    step = (-1, 1)

    def x_dev(s):
        return there["gx"][s], {"gx": gx + step[s]}

    def y_dev(s):
        return there["gy"][s], {"gy": gy + step[s]}

    def c_dev(sx, sy):
        return (
            jnp.logical_and(there["gx"][sx], there["gy"][sy]),
            {"gx": gx + step[sx], "gy": gy + step[sy]},
        )

    class Exchange:
        def __init__(self, send, recv):
            self.items = []
            self.send = send
            self.recv = recv

        def add(self, where, src, dst, mine, out_slot, in_slot):
            cond, dev = where
            n = len(self.items)
            copy = pltpu.make_async_remote_copy(
                src_ref=src,
                dst_ref=dst,
                send_sem=self.send.at[n],
                recv_sem=self.recv.at[out_slot],
                device_id=dev,
                device_id_type=MESH,
            )
            back = pltpu.make_async_remote_copy(
                src_ref=src,
                dst_ref=mine,
                send_sem=self.send.at[n],
                recv_sem=self.recv.at[in_slot],
                device_id=dev,
                device_id_type=MESH,
            )
            self.items.append((cond, copy, back))

        def start(self):
            for cond, copy, _ in self.items:
                pl.when(cond)(copy.start)

        def finish(self):
            for cond, copy, back in self.items:

                @pl.when(cond)
                def _():
                    back.wait_recv()
                    copy.wait_send()

    rows = ny + 2 * OY

    def clear(xp, carry):
        zero = jnp.zeros((rows, nz), jnp.float32)
        for f in range(4):
            state[1, f, xp] = zero
        state[0, 3, xp] = zero
        held[xp] = zero
        pinned[xp] = zero + 1.0
        free[xp] = zero
        return carry

    lax.fori_loop(0, nx + 2 * HX, clear, 0)

    for copy in fetch:
        copy.wait()

    pack_mask[0, :, 0:3, :] = load_ref[:, 0:3, :]
    pack_mask[0, :, 3:5, :] = crack_ref[:, 0:2, :]
    pack_mask[0, :, 5:6, :] = clamp_ref[:, 0:1, :]
    pack_mask[1, :, 0:3, :] = load_ref[:, ny - 3 : ny, :]
    pack_mask[1, :, 3:5, :] = crack_ref[:, ny - 2 : ny, :]
    pack_mask[1, :, 5:6, :] = clamp_ref[:, ny - 1 : ny, :]

    pl.semaphore_wait(barrier, group - 1 + sections - 1)

    masks = Exchange(mask_send, mask_recv)
    for s in range(2):
        for j, (ref, width, at) in enumerate(
            ((load_ref, 3, 0), (crack_ref, 2, 3), (clamp_ref, 1, 5))
        ):
            first = 0 if s == 0 else nx - width
            masks.add(
                x_dev(s),
                ref.at[pl.ds(first, width)],
                in_mask_x.at[1 - s, pl.ds(at, width)],
                in_mask_x.at[s, pl.ds(at, width)],
                (1 - s) * 3 + j,
                s * 3 + j,
            )
    for s in range(2):
        masks.add(
            y_dev(s), pack_mask.at[s], in_mask_y.at[1 - s], in_mask_y.at[s], 6 + 1 - s, 6 + s
        )
    for sx in range(2):
        for sy in range(2):
            masks.add(
                c_dev(sx, sy),
                pack_mask.at[sy, pl.ds(0 if sx == 0 else nx - 2, 2)],
                in_mask_c.at[(1 - sx) * 2 + 1 - sy],
                in_mask_c.at[sx * 2 + sy],
                8 + (1 - sx) * 2 + 1 - sy,
                8 + sx * 2 + sy,
            )
    masks.start()

    tough_copies = []
    for k in range(1, sections):
        copy = pltpu.make_async_remote_copy(
            src_ref=tough_ref.at[0],
            dst_ref=tough_in.at[k - 1],
            send_sem=tough_send.at[k - 1],
            recv_sem=tough_recv.at[k - 1],
            device_id={"section": lax.rem(sec + sections - k, sections)},
            device_id_type=MESH,
        )
        copy.start()
        tough_copies.append(copy)

    inner = slice(OY, OY + ny)

    def fill(x, carry):
        load = load_ref[x].astype(jnp.float32)
        fixed = jnp.maximum(clamp_ref[x].astype(jnp.float32), load)
        held[x + HX, inner] = load
        pinned[x + HX, inner] = fixed
        free[x + HX, inner] = 1.0 - fixed
        state[0, 3, x + HX, inner] = crack_ref[x].astype(jnp.float32)
        return carry

    lax.fori_loop(0, nx, fill, 0)

    case = index_ref[0]
    vector = [table_ref[f, case] for f in range(3)]

    masks.finish()
    as_float = lambda v: v.astype(jnp.float32)
    planes = slice(HX, HX + nx)
    x_far = (slice(HX - 3, HX), slice(HX + nx, HX + nx + 3))
    x_two = (slice(HX - 2, HX), slice(HX + nx, HX + nx + 2))
    x_one = (slice(HX - 1, HX), slice(HX + nx, HX + nx + 1))
    y_far = (slice(OY - 3, OY), slice(OY + ny, OY + ny + 3))
    y_two = (slice(OY - 2, OY), slice(OY + ny, OY + ny + 2))
    y_one = (slice(OY - 1, OY), slice(OY + ny, OY + ny + 1))
    for s in range(2):

        @pl.when(there["gx"][s])
        def _(s=s):
            load = as_float(in_mask_x[s, 0:3])
            near = slice(2, 3) if s == 0 else slice(0, 1)
            held[x_far[s], inner] = load
            state[0, 3, x_two[s], inner] = as_float(in_mask_x[s, 3:5])
            pinned[x_one[s], inner] = jnp.maximum(load[near], as_float(in_mask_x[s, 5:6]))

        @pl.when(there["gy"][s])
        def _(s=s):
            held[planes, y_far[s]] = as_float(in_mask_y[s, :, 0:3])
            state[0, 3, planes, y_two[s]] = as_float(in_mask_y[s, :, 3:5])
            near = slice(2, 3) if s == 0 else slice(0, 1)
            pinned[planes, y_one[s]] = jnp.maximum(
                as_float(in_mask_y[s, :, near]), as_float(in_mask_y[s, :, 5:6])
            )

    for sx in range(2):
        for sy in range(2):

            @pl.when(c_dev(sx, sy)[0])
            def _(sx=sx, sy=sy):
                near = slice(1, 3) if sy == 0 else slice(0, 2)
                held[x_two[sx], y_two[sy]] = as_float(in_mask_c[sx * 2 + sy, :, near])
                state[0, 3, x_two[sx], y_two[sy]] = as_float(in_mask_c[sx * 2 + sy, :, 3:5])

    def begin(xp, carry):
        load = held[xp]
        for f in range(3):
            state[0, f, xp] = load * vector[f]
        return carry

    lax.fori_loop(0, nx + 2 * HX, begin, 0)

    wide = up8(ny + 4)
    near = up8(ny + 2)

    def lanes(shape, lane):
        return lax.broadcasted_iota(jnp.int32, shape, 1) == lane

    def beside(v, edge, first, last):
        up = jnp.where(last, edge, pltpu.roll(v, nz - 1, 1))
        down = jnp.where(first, edge, pltpu.roll(v, 1, 1))
        return up, down

    def sweep(rnd):
        p = rnd % 2
        q = 1 - p
        done = rnd == sections - 1
        tough = tough_ref.at[0] if rnd == 0 else tough_in.at[rnd - 1]

        shape = (wide, nz)
        first, last = lanes(shape, 0), lanes(shape, nz - 1)
        row = lax.broadcasted_iota(jnp.int32, shape, 0) + (gy * ny - 2)
        row_inside = jnp.logical_and(row >= 0, row < ny * ngy)
        a = OY - 2

        def stiffen(xp, carry):
            d = state[p, 3, xp, a : a + wide]
            half = 0.5 * (jnp.square(1.0 - d) + stiff_floor)
            stiff[xp, a : a + wide] = half
            up, down = beside(state[p, 2, xp, a : a + wide], 0.0, first, last)
            div = (
                (state[p, 0, xp + 1, a : a + wide] - state[p, 0, xp - 1, a : a + wide])
                + (state[p, 1, xp, a + 1 : a + 1 + wide] - state[p, 1, xp, a - 1 : a - 1 + wide])
                + (up - down)
            )
            plane = xp - HX + gx * nx
            ok = jnp.logical_and(plane >= 0, plane < nx * ngx)
            flow[xp, a : a + wide] = jnp.where(
                jnp.logical_and(row_inside, ok), half * div, 0.0
            )
            return carry

        lax.fori_loop(HX - 2, HX + nx + 2, stiffen, 0, unroll=2 if nx % 2 == 0 else 1)

        shape = (near, nz)
        first, last = lanes(shape, 0), lanes(shape, nz - 1)
        b = OY - 1

        def move(xp, total):
            at = lambda ref, dx, dy: ref[xp + dx, b + dy : b + dy + near]
            k = at(stiff, 0, 0)
            edge = 0.5 * (1.0 + stiff_floor)
            kz = beside(k, edge, first, last)
            kx = (at(stiff, 1, 0), at(stiff, -1, 0))
            ky = (at(stiff, 0, 1), at(stiff, 0, -1))
            sides = (kx, ky, kz)
            pairs = [s[0] + s[1] for s in sides]
            weights = pairs[0] + pairs[1] + pairs[2] + 6.0 * k
            faces = [(k + s[0], k + s[1]) for s in sides]
            grads = (
                at(flow, 1, 0) - at(flow, -1, 0),
                at(flow, 0, 1) - at(flow, 0, -1),
                None,
            )
            fz = beside(at(flow, 0, 0), 0.0, first, last)
            grads = (grads[0], grads[1], fz[0] - fz[1])
            pin = at(pinned, 0, 0) > 0.5
            load = at(held, 0, 0)
            squares = None
            for f in range(3):
                u = state.at[p, f]
                here = at(u, 0, 0)
                uz = beside(here, 0.0, first, last)
                res = (
                    faces[0][0] * at(u, 1, 0)
                    + faces[0][1] * at(u, -1, 0)
                    + faces[1][0] * at(u, 0, 1)
                    + faces[1][1] * at(u, 0, -1)
                    + faces[2][0] * uz[0]
                    + faces[2][1] * uz[1]
                    - weights * here
                    + grads[f]
                )
                moved = here + relax_weight * res / (weights + pairs[f])
                state[q, f, xp, b : b + near] = jnp.where(pin, load * vector[f], moved)
                square = res * res
                squares = square if squares is None else squares + square
            return total + jnp.where(at(free, 0, 0) > 0.5, squares, 0.0)

        total = lax.fori_loop(HX - 1, HX + nx + 1, move, jnp.zeros(shape, jnp.float32))
        sums[rnd, me] = jnp.sum(total, axis=0, keepdims=True)
        par = rnd % 2
        if not done:
            for f in range(3):
                pack_u[0, :, 2 * f : 2 * f + 2] = state[q, f, planes, OY : OY + 2]
                pack_u[1, :, 2 * f : 2 * f + 2] = state[q, f, planes, OY + ny - 2 : OY + ny]
            pack_u[0, :, 6:7] = state[q, 1, planes, OY + 2 : OY + 3]
            pack_u[1, :, 6:7] = state[q, 1, planes, OY + ny - 3 : OY + ny - 2]
            shift = Exchange(u_send, u_recv.at[par])
            mid = pl.ds(OY, ny)
            for s in range(2):
                shift.add(
                    x_dev(s),
                    state.at[q, pl.ds(0, 3), pl.ds(HX if s == 0 else HX + nx - 2, 2), mid],
                    in_u_x.at[par, 1 - s],
                    in_u_x.at[par, s],
                    (1 - s),
                    s,
                )
                shift.add(
                    x_dev(s),
                    state.at[q, 0, HX + 2 if s == 0 else HX + nx - 3, mid],
                    in_u_x3.at[par, 1 - s],
                    in_u_x3.at[par, s],
                    2 + (1 - s),
                    2 + s,
                )
            for s in range(2):
                shift.add(
                    y_dev(s),
                    pack_u.at[s],
                    in_u_y.at[par, 1 - s],
                    in_u_y.at[par, s],
                    4 + (1 - s),
                    4 + s,
                )
            for sx in range(2):
                for sy in range(2):
                    shift.add(
                        c_dev(sx, sy),
                        pack_u.at[sy, pl.ds(0 if sx == 0 else nx - 2, 2)],
                        in_u_c.at[par, (1 - sx) * 2 + 1 - sy],
                        in_u_c.at[par, sx * 2 + sy],
                        6 + (1 - sx) * 2 + 1 - sy,
                        6 + sx * 2 + sy,
                    )
            shift.start()

        for k, peer in enumerate(peers):
            pltpu.make_async_remote_copy(
                src_ref=sums.at[rnd, me],
                dst_ref=sums.at[rnd, me],
                send_sem=sum_send.at[rnd, k],
                recv_sem=sum_recv.at[rnd, me],
                device_id=peer,
                device_id_type=MESH,
            ).start()

        if rnd > 0:
            tough_copies[rnd - 1].wait_recv()

        shape = (ny, nz)
        first, last = lanes(shape, 0), lanes(shape, nz - 1)

        def damage(x, carry):
            xp = x + HX
            at = lambda ref, dx, dy: ref[xp + dx, OY + dy : OY + dy + ny]
            grad = []
            for f in range(3):
                u = state.at[q, f]
                here = at(u, 0, 0)
                uz = beside(here, 0.0, first, last)
                grad.append(
                    (at(u, 1, 0) - at(u, -1, 0), at(u, 0, 1) - at(u, 0, -1), uz[0] - uz[1])
                )
                if done:
                    disp_refs[f][x] = here
            energy = 2.0 * spectral_energy(
                0.5 * grad[0][0],
                0.5 * grad[1][1],
                0.5 * grad[2][2],
                0.25 * (grad[0][1] + grad[1][0]),
                0.25 * (grad[0][2] + grad[2][0]),
                0.25 * (grad[1][2] + grad[2][1]),
            )
            d = state.at[p, 3]
            dz = beside(at(d, 0, 0), 0.0, first, last)
            around = (
                at(d, 1, 0) + at(d, -1, 0) + at(d, 0, 1) + at(d, 0, -1) + dz[0] + dz[1]
            )
            g = tough[x]
            renewed = (energy + g * around) / (7.0 * g + energy)
            renewed = jnp.where(crack_ref[x] > 0, 1.0, renewed)
            if done:
                dam_ref[x] = renewed
            else:
                state[q, 3, xp, inner] = renewed
            return carry

        lax.fori_loop(0, nx, damage, 0, unroll=4 if nx % 4 == 0 else 1)
        if done:
            return

        pack_d[0] = state[q, 3, planes, OY : OY + 2]
        pack_d[1] = state[q, 3, planes, OY + ny - 2 : OY + ny]
        crack = Exchange(d_send, d_recv.at[par])
        for s in range(2):
            crack.add(
                x_dev(s),
                state.at[q, 3, pl.ds(HX if s == 0 else HX + nx - 2, 2), mid],
                in_d_x.at[par, 1 - s],
                in_d_x.at[par, s],
                1 - s,
                s,
            )
        for s in range(2):
            crack.add(
                y_dev(s),
                pack_d.at[s],
                in_d_y.at[par, 1 - s],
                in_d_y.at[par, s],
                2 + 1 - s,
                2 + s,
            )
        for sx in range(2):
            for sy in range(2):
                crack.add(
                    c_dev(sx, sy),
                    pack_d.at[sy, pl.ds(0 if sx == 0 else nx - 1, 1)],
                    in_d_c.at[par, (1 - sx) * 2 + 1 - sy],
                    in_d_c.at[par, sx * 2 + sy],
                    4 + (1 - sx) * 2 + 1 - sy,
                    4 + sx * 2 + sy,
                )
        crack.start()
        shift.finish()
        third_x = (HX - 3, HX + nx + 2)
        third_y = (slice(OY - 3, OY - 2), slice(OY + ny + 2, OY + ny + 3))
        for s in range(2):

            @pl.when(there["gx"][s])
            def _(s=s):
                state[q, 0:3, x_two[s], inner] = in_u_x[par, s]
                state[q, 0, third_x[s], inner] = in_u_x3[par, s]

            @pl.when(there["gy"][s])
            def _(s=s):
                for f in range(3):
                    state[q, f, planes, y_two[s]] = in_u_y[par, s, :, 2 * f : 2 * f + 2]
                state[q, 1, planes, third_y[s]] = in_u_y[par, s, :, 6:7]

        for sx in range(2):
            for sy in range(2):

                @pl.when(c_dev(sx, sy)[0])
                def _(sx=sx, sy=sy):
                    for f in range(3):
                        state[q, f, x_two[sx], y_two[sy]] = in_u_c[
                            par, sx * 2 + sy, :, 2 * f : 2 * f + 2
                        ]

        crack.finish()
        for s in range(2):

            @pl.when(there["gx"][s])
            def _(s=s):
                state[q, 3, x_two[s], inner] = in_d_x[par, s]

            @pl.when(there["gy"][s])
            def _(s=s):
                state[q, 3, planes, y_two[s]] = in_d_y[par, s]

        for sx in range(2):
            for sy in range(2):

                @pl.when(c_dev(sx, sy)[0])
                def _(sx=sx, sy=sy):
                    state[q, 3, x_one[sx], y_two[sy]] = in_d_c[par, sx * 2 + sy]

    for rnd in range(sections):
        sweep(rnd)

    cells = 3.0 * nx * ngx * ny * ngy * nz
    column = lax.broadcasted_iota(jnp.int32, (1, sections), 1)
    norms = jnp.zeros((1, sections), jnp.float32)
    for rnd in range(sections):
        for k in range(1, group):
            other = lax.rem(me + k, group)
            pltpu.make_async_remote_copy(
                src_ref=sums.at[rnd, me],
                dst_ref=sums.at[rnd, other],
                send_sem=sum_send.at[rnd, k - 1],
                recv_sem=sum_recv.at[rnd, other],
                device_id=peers[k - 1],
                device_id_type=MESH,
            ).wait()
        total = sums[rnd, 0]
        for k in range(1, group):
            total = total + sums[rnd, k]
        entry = jnp.sqrt(jnp.sum(total, axis=1, keepdims=True) / cells)
        norms = jnp.where(column == lax.rem(sec + rnd, sections), entry, norms)
    norm_ref[...] = norms
    for copy in tough_copies:
        copy.wait_send()


def put_out(
    first_ref, second_ref, third_ref, dam_ref, norm_ref, disp_hbm, dam_hbm, norm_out, sems
):
    copies = [
        pltpu.make_async_copy(ref, disp_hbm.at[0, f], sems.at[f])
        for f, ref in enumerate((first_ref, second_ref, third_ref))
    ]
    copies.append(pltpu.make_async_copy(dam_ref, dam_hbm.at[0], sems.at[3]))
    for copy in copies:
        copy.start()
    norm_out[...] = norm_ref[...]
    for copy in copies:
        copy.wait()


def on_device(sizes, load_index, load_table, toughness, clamp_mask, load_mask, crack_mask):
    sections, ngx, ngy = sizes
    nx, ny, nz = clamp_mask.shape
    assert load_index.shape == (1,)
    group = ngx * ngy
    f32 = jnp.float32
    padded = (nx + 2 * HX, ny + 2 * OY, nz)
    vmem = pltpu.VMEM
    dma = pltpu.SemaphoreType.DMA
    later = max(sections - 1, 1)
    scratch = [
        pltpu.SMEM(load_index.shape, jnp.int32),
        pltpu.SMEM(load_table.shape[::-1], f32),
        vmem((1, nx, ny, nz), f32),
        vmem((nx, ny, nz), jnp.int32),
        vmem((nx, ny, nz), jnp.int32),
        vmem((nx, ny, nz), jnp.int32),
        dma((6,)),
        vmem((2, 4) + padded, f32),
        vmem(padded, f32),
        vmem(padded, f32),
        vmem(padded, f32),
        vmem(padded, f32),
        vmem(padded, f32),
        vmem((later, nx, ny, nz), f32),
        vmem((2, nx, 8, nz), jnp.int32),
        vmem((2, nx, 8, nz), f32),
        vmem((2, nx, 2, nz), f32),
        vmem((2, 6, ny, nz), jnp.int32),
        vmem((2, nx, 8, nz), jnp.int32),
        vmem((4, 2, 8, nz), jnp.int32),
        vmem((2, 2, 3, 2, ny, nz), f32),
        vmem((2, 2, ny, nz), f32),
        vmem((2, 2, nx, 8, nz), f32),
        vmem((2, 4, 2, 8, nz), f32),
        vmem((2, 2, 2, ny, nz), f32),
        vmem((2, 2, nx, 2, nz), f32),
        vmem((2, 4, 1, 2, nz), f32),
        vmem((sections, group, 1, nz), f32),
        dma((12,)),
        dma((12,)),
        dma((10,)),
        dma((2, 10)),
        dma((8,)),
        dma((2, 8)),
        dma((later,)),
        dma((later,)),
        dma((sections, max(group - 1, 1))),
        dma((sections, group)),
    ]
    block = pl.BlockSpec(memory_space=pltpu.VMEM)
    away = pl.BlockSpec(memory_space=pltpu.HBM)
    results = pl.pallas_call(
        functools.partial(kernel, (sections, ngx, ngy, nx, ny, nz)),
        out_shape=(
            *[jax.ShapeDtypeStruct((nx, ny, nz), f32)] * 4,
            jax.ShapeDtypeStruct((1, sections), f32),
        ),
        in_specs=[away] * 6,
        out_specs=(block,) * 5,
        scratch_shapes=scratch,
        compiler_params=pltpu.CompilerParams(
            collective_id=0, has_side_effects=True, vmem_limit_bytes=56_020_000
        ),
    )(load_index, load_table.T, toughness, clamp_mask, load_mask, crack_mask)
    return pl.pallas_call(
        put_out,
        out_shape=(
            jax.ShapeDtypeStruct((1, 3, nx, ny, nz), f32),
            jax.ShapeDtypeStruct((1, nx, ny, nz), f32),
            jax.ShapeDtypeStruct((1, sections), f32),
        ),
        in_specs=[block] * 5,
        out_specs=(away, away, block),
        scratch_shapes=[dma((4,))],
        compiler_params=pltpu.CompilerParams(vmem_limit_bytes=1024 * 1024),
    )(*results)


def solution(mesh):
    in_specs = (
        P("section"),
        P(),
        P("section", "gx", "gy", None),
        P("gx", "gy", None),
        P("gx", "gy", None),
        P("gx", "gy", None),
    )
    out_specs = (
        P("section", None, "gx", "gy", None),
        P("section", "gx", "gy", None),
        P("section", None),
    )
    sizes = tuple(mesh.shape[name] for name in ("section", "gx", "gy"))
    return jax.shard_map(
        functools.partial(on_device, sizes),
        mesh=mesh,
        in_specs=in_specs,
        out_specs=out_specs,
        check_vma=False,
    )
```

profile of v0, /device:TPU:0, one launch (start us, length us, event | category | flops | bytes accessed | tf_op | source)
XLA Modules:
  0.0 26.9 jit_solution(16311711805115833707)
XLA Ops:
  0.6 0.0 copy-start
  1.3 0.0 copy-done
  1.3 24.3 %shard_map.85 = (f32[16,16,128]{2,1,0:T(8,128)S(1)}, f32[16,16,128]{2,1,0:T(8,128)S(1)}, f32[16,16,128]{2,1,0:T(8,128)S(1)}, f32[16,16,128]{2,1,0:T(8,128)S(1)}, f32[1,2]{1,0:T(1,128)S(1)}) custom-call(s32[1]{0:T(128)S(6)} %copy.9.index_hbm, f32[3,64]{1,0:T(4,128)S(1)} %bitcast.1, f32[1,16,16,128]{3,2,1,0:T(8,128)} %tough_hbm.1, s32[16,16,128]{2,1,0:T(8,128)} %clamp_hbm.1, ...), custom_call_target="tpu_custom_call" | custom-call | tf_op jit(solution)/shard_map/pallas_call | solution.py:712
  25.6 1.3 %shard_map.86 = (f32[1,3,16,16,128]{4,3,2,1,0:T(8,128)}, f32[1,16,16,128]{3,2,1,0:T(8,128)}, f32[1,2]{1,0:T(1,128)}) custom-call(f32[16,16,128]{2,1,0:T(8,128)S(1)} %get-tuple-element.8.first_ref, f32[16,16,128]{2,1,0:T(8,128)S(1)} %get-tuple-element.9.second_ref, f32[16,16,128]{2,1,0:T(8,128)S(1)} %get-tuple-element.10.third_ref, ...), custom_call_target="tpu_custom_call" | custom-call | tf_op jit(solution)/shard_map/pallas_call | solution.py:725
Async XLA Ops:
  0.6 0.7 %copy-start = (f32[64,3]{0,1:T(4,128)S(1)}, f32[64,3]{0,1:T(4,128)}, u32[]{:S(2)}) copy-start(f32[64,3]{0,1:T(4,128)} %param.7) | copy-start | bytes 2308
where the time goes:
time: 27.1 us; the launch traced here: 26.9 us
  Pallas kernels  25.6 us (94%)
  between operations  1.31 us (5%)
    pallas_call x1, Pallas kernels, on_device(): pl.pallas_call(functools.partial(kernel, (sections, ngx, ngy, nx, ny, nz)...  24.3 us
    pallas_call x1, Pallas kernels, on_device(): pl.pallas_call(put_out, out_shape=(jax.ShapeDtypeStruct((1, 3, nx, ny, nz...  1.33 us

commit v1 on v0

--- a/solution.py
+++ b/solution.py
@@ -30,6 +30,10 @@
 
 def up8(n):
     return -(-n // 8) * 8
+
+
+def part(n, most):
+    return max(k for k in range(1, most + 1) if n % k == 0)
 
 
 def spectral_energy(xx, yy, zz, xy, xz, yz):
@@ -388,7 +392,7 @@
             )
             return carry
 
-        lax.fori_loop(HX - 2, HX + nx + 2, stiffen, 0, unroll=2 if nx % 2 == 0 else 1)
+        lax.fori_loop(HX - 2, HX + nx + 2, stiffen, 0, unroll=part(nx + 4, 10))
 
         shape = (near, nz)
         first, last = lanes(shape, 0), lanes(shape, nz - 1)
@@ -435,7 +439,9 @@
                 squares = square if squares is None else squares + square
             return total + jnp.where(at(free, 0, 0) > 0.5, squares, 0.0)
 
-        total = lax.fori_loop(HX - 1, HX + nx + 1, move, jnp.zeros(shape, jnp.float32))
+        total = lax.fori_loop(
+            HX - 1, HX + nx + 1, move, jnp.zeros(shape, jnp.float32), unroll=part(nx + 2, 6)
+        )
         sums[rnd, me] = jnp.sum(total, axis=0, keepdims=True)
         par = rnd % 2
         if not done:
@@ -535,7 +541,7 @@
                 state[q, 3, xp, inner] = renewed
             return carry
 
-        lax.fori_loop(0, nx, damage, 0, unroll=4 if nx % 4 == 0 else 1)
+        lax.fori_loop(0, nx, damage, 0, unroll=part(nx, 8))
         if done:
             return
 

time: 27.1 us -> 23.9 us (0.88)
  Pallas kernels: 25.6 us -> 22.4 us
    pallas_call x1, Pallas kernels: 24.3 us -> 21.1 us  [on_device(): pl.pallas_call(functools.partial(kernel, (sections, ngx, ngy, nx, ny, nz)...]
where the time goes in v1:
time: 23.9 us; the launch traced here: 23.7 us
  Pallas kernels  22.4 us (94%)
  between operations  1.31 us (5%)
    pallas_call x1, Pallas kernels, on_device(): pl.pallas_call(functools.partial(kernel, (sections, ngx, ngy, nx, ny, nz)...  21.1 us
    pallas_call x1, Pallas kernels, on_device(): pl.pallas_call(put_out, out_shape=(jax.ShapeDtypeStruct((1, 3, nx, ny, nz...  1.33 us

profile of v1, /device:TPU:0, one launch (start us, length us, event | category | flops | bytes accessed | tf_op | source)
XLA Modules:
  0.0 23.7 jit_solution(622511114961148591)
XLA Ops:
  0.6 0.0 copy-start
  1.3 0.0 copy-done
  1.3 21.1 %shard_map.85 = (f32[16,16,128]{2,1,0:T(8,128)S(1)}, f32[16,16,128]{2,1,0:T(8,128)S(1)}, f32[16,16,128]{2,1,0:T(8,128)S(1)}, f32[16,16,128]{2,1,0:T(8,128)S(1)}, f32[1,2]{1,0:T(1,128)S(1)}) custom-call(s32[1]{0:T(128)S(6)} %copy.9.index_hbm, f32[3,64]{1,0:T(4,128)S(1)} %bitcast.1, f32[1,16,16,128]{3,2,1,0:T(8,128)} %tough_hbm.1, s32[16,16,128]{2,1,0:T(8,128)} %clamp_hbm.1, ...), custom_call_target="tpu_custom_call" | custom-call | tf_op jit(solution)/shard_map/pallas_call | solution.py:718
  22.4 1.3 %shard_map.86 = (f32[1,3,16,16,128]{4,3,2,1,0:T(8,128)}, f32[1,16,16,128]{3,2,1,0:T(8,128)}, f32[1,2]{1,0:T(1,128)}) custom-call(f32[16,16,128]{2,1,0:T(8,128)S(1)} %get-tuple-element.8.first_ref, f32[16,16,128]{2,1,0:T(8,128)S(1)} %get-tuple-element.9.second_ref, f32[16,16,128]{2,1,0:T(8,128)S(1)} %get-tuple-element.10.third_ref, ...), custom_call_target="tpu_custom_call" | custom-call | tf_op jit(solution)/shard_map/pallas_call | solution.py:731
Async XLA Ops:
  0.6 0.7 %copy-start = (f32[64,3]{0,1:T(4,128)S(1)}, f32[64,3]{0,1:T(4,128)}, u32[]{:S(2)}) copy-start(f32[64,3]{0,1:T(4,128)} %param.7) | copy-start | bytes 2308

commit v2 on v1

v2 whole, which is shorter than its diff:
```python
import functools
import math
import types

import jax
import jax.numpy as jnp
from jax import lax
from jax.experimental import pallas as pl
from jax.experimental.pallas import tpu as pltpu
from jax.sharding import PartitionSpec as P

relax_weight = 0.6
stiff_floor = 0.001
eigen_guard = 1e-08
MESH = pl.DeviceIdType.MESH

HX = 5
OY = 8

ACOS = (
    1.5707963050,
    -0.2145988016,
    0.0889789874,
    -0.0501743046,
    0.0308918810,
    -0.0170881256,
    0.0066700901,
    -0.0012624911,
)


def up8(n):
    return -(-n // 8) * 8


def part(n, most):
    return max(k for k in range(1, most + 1) if n % k == 0)


def root(v):
    return v * lax.rsqrt(jnp.maximum(v, 1.2e-38))


def spectral_energy(xx, yy, zz, xy, xz, yz):
    trace = xx + yy + zz
    mid = trace * (1.0 / 3.0)
    dx = xx - mid
    dy = yy - mid
    dz = zz - mid
    xy2 = xy * xy
    xz2 = xz * xz
    yz2 = yz * yz
    sixth = (dx * dx + dy * dy + dz * dz + 2.0 * (xy2 + xz2 + yz2)) * (1.0 / 6.0)
    twice_radius = 2.0 * root(sixth)
    scale = lax.rsqrt(sixth + eigen_guard)
    det = dx * (dy * dz - yz2) - dz * xy2 - dy * xz2 + 2.0 * (xy * xz * yz)
    ratio = (0.5 * det * scale) * (scale * scale)
    size = jnp.minimum(jnp.abs(ratio), 1.0)
    poly = jnp.full_like(size, ACOS[-1] / 3.0)
    for c in ACOS[-2::-1]:
        poly = poly * size + c / 3.0
    t = root(1.0 - size) * poly
    t2 = t * t
    cos_t = 1.0 + t2 * (-0.5 + t2 * (1.0 / 24.0 + t2 * (-1.0 / 720.0 + t2 * (1.0 / 40320.0))))
    sin_t = t * (1.0 + t2 * (-1.0 / 6.0 + t2 * (1.0 / 120.0 + t2 * (-1.0 / 5040.0))))
    other = 0.5 * cos_t + math.sqrt(0.75) * sin_t
    upper = ratio >= 0.0
    first = jnp.where(upper, cos_t, other)
    last = jnp.where(upper, other, cos_t)
    largest = mid + twice_radius * first
    smallest = mid - twice_radius * last
    between = trace - largest - smallest
    relu = lambda v: jnp.maximum(v, 0.0)
    return (
        0.5 * jnp.square(relu(trace))
        + jnp.square(relu(largest))
        + jnp.square(relu(between))
        + jnp.square(relu(smallest))
    )


def kernel(sizes, names, *refs):
    sections, ngx, ngy, nx, ny, nz = sizes
    r = types.SimpleNamespace(**dict(zip(names, refs)))
    local, state, stiff, flow = r.local, r.state, r.stiff, r.flow
    held, clamped, free, tough_pad, crack_pad = r.held, r.clamped, r.free, r.tough_pad, r.crack_pad
    load_ref, crack_ref, clamp_ref, tough_ref = r.load_ref, r.crack_ref, r.clamp_ref, r.tough_ref
    disp_refs = (r.first_ref, r.second_ref, r.third_ref)
    sec = lax.axis_index("section")
    gx = lax.axis_index("gx")
    gy = lax.axis_index("gy")
    group = ngx * ngy
    me = gx * ngy + gy
    peers = []
    for k in range(1, group):
        other = lax.rem(me + k, group)
        peers.append({"gx": other // ngy, "gy": lax.rem(other, ngy)})

    fetch = [
        pltpu.make_async_copy(src, dst, local.at[n])
        for n, (src, dst) in enumerate(
            (
                (r.load_hbm, load_ref),
                (r.crack_hbm, crack_ref),
                (r.clamp_hbm, clamp_ref),
                (r.tough_hbm, tough_ref),
                (r.index_hbm, r.index_ref),
                (r.table_hbm, r.table_ref),
            )
        )
    ]
    for copy in fetch:
        copy.start()

    barrier = pltpu.get_barrier_semaphore()
    for peer in peers:
        pl.semaphore_signal(barrier, inc=1, device_id=peer, device_id_type=MESH)
    for k in range(1, sections):
        pl.semaphore_signal(
            barrier,
            inc=1,
            device_id={"section": lax.rem(sec + k, sections)},
            device_id_type=MESH,
        )

    there = {
        "gx": (gx > 0, gx < ngx - 1),
        "gy": (gy > 0, gy < ngy - 1),
    }
    step = (-1, 1)

    def x_dev(s):
        return there["gx"][s], {"gx": gx + step[s]}

    def y_dev(s):
        return there["gy"][s], {"gy": gy + step[s]}

    def c_dev(sx, sy):
        return (
            jnp.logical_and(there["gx"][sx], there["gy"][sy]),
            {"gx": gx + step[sx], "gy": gy + step[sy]},
        )

    class Exchange:
        def __init__(self, send, recv):
            self.items = []
            self.send = send
            self.recv = recv

        def add(self, where, src, dst, mine, out_slot, in_slot):
            cond, dev = where
            n = len(self.items)
            copy = pltpu.make_async_remote_copy(
                src_ref=src,
                dst_ref=dst,
                send_sem=self.send.at[n],
                recv_sem=self.recv.at[out_slot],
                device_id=dev,
                device_id_type=MESH,
            )
            back = pltpu.make_async_remote_copy(
                src_ref=src,
                dst_ref=mine,
                send_sem=self.send.at[n],
                recv_sem=self.recv.at[in_slot],
                device_id=dev,
                device_id_type=MESH,
            )
            self.items.append((cond, copy, back))

        def start(self):
            for cond, copy, _ in self.items:
                pl.when(cond)(copy.start)

        def finish(self):
            for cond, copy, back in self.items:

                @pl.when(cond)
                def _():
                    back.wait_recv()
                    copy.wait_send()

        def received(self):
            for cond, _, back in self.items:
                pl.when(cond)(back.wait_recv)

        def sent(self):
            for cond, copy, _ in self.items:
                pl.when(cond)(copy.wait_send)

    rows = ny + 2 * OY

    def clear(xp, carry):
        zero = jnp.zeros((rows, nz), jnp.float32)
        held[xp] = zero
        crack_pad[xp] = zero
        clamped[xp] = zero + 1.0
        tough_pad[xp] = zero + 1.0
        free[xp] = zero
        if sections > 2:
            for p in range(2):
                for f in range(4):
                    state[p, f, xp] = zero
        return carry

    lax.fori_loop(0, nx + 2 * HX, clear, 0)

    for copy in fetch[:3]:
        copy.wait()

    for s in range(2):
        side = lambda n, s=s: slice(0, n) if s == 0 else slice(ny - n, ny)
        r.pack_l[s, :, 0:5] = load_ref[:, side(5)]
        r.pack_l[s, :, 5:8] = clamp_ref[:, side(3)]
        r.pack_c[s] = crack_ref[:, side(4)]
    corner = (
        (load_ref, held, 1, 4, 0),
        (load_ref, held, 2, 3, 4),
        (load_ref, held, 4, 1, 7),
        (load_ref, held, 3, 2, 8),
        (crack_ref, crack_pad, 1, 3, 10),
        (crack_ref, crack_pad, 2, 2, 13),
        (crack_ref, crack_pad, 3, 1, 15),
        (clamp_ref, clamped, 1, 2, 16),
        (clamp_ref, clamped, 2, 1, 18),
    )
    for sx in range(2):
        for sy in range(2):
            for ref, _, deep, n, at in corner:
                plane = deep - 1 if sx == 0 else nx - deep
                first = 0 if sy == 0 else ny - n
                r.pack_k[sx * 2 + sy, at // 8, at % 8 : at % 8 + n] = ref[plane, first : first + n]

    pl.semaphore_wait(barrier, group - 1 + sections - 1)

    early = Exchange(r.early_send, r.early_recv)
    later = Exchange(r.later_send, r.later_recv)
    last_one = Exchange(r.last_send, r.last_recv)
    for s in range(2):
        for ex, ref, buf, width, at, slot in (
            (early, load_ref, r.in_x, 5, 0, 0),
            (early, crack_ref, r.in_x, 4, 5, 2),
            (later, clamp_ref, r.in_x, 3, 9, 0),
            (last_one, tough_ref.at[0], r.in_tx, 2, 0, 0),
        ):
            ex.add(
                x_dev(s),
                ref.at[pl.ds(0 if s == 0 else nx - width, width)],
                buf.at[1 - s, pl.ds(at, width)],
                buf.at[s, pl.ds(at, width)],
                slot + 1 - s,
                slot + s,
            )
    for s in range(2):
        for ex, pack, buf, slot in (
            (early, r.pack_l, r.in_l, 4),
            (early, r.pack_c, r.in_c, 6),
            (last_one, r.pack_t, r.in_ty, 2),
        ):
            ex.add(
                y_dev(s), pack.at[s], buf.at[1 - s], buf.at[s], slot + 1 - s, slot + s
            )
    for sx in range(2):
        for sy in range(2):
            here, away = sx * 2 + sy, (1 - sx) * 2 + 1 - sy
            early.add(
                c_dev(sx, sy), r.pack_k.at[here], r.in_k.at[away], r.in_k.at[here],
                8 + away, 8 + here,
            )
            last_one.add(
                c_dev(sx, sy), r.pack_tk.at[here], r.in_tk.at[away], r.in_tk.at[here],
                4 + away, 4 + here,
            )
    early.start()
    later.start()

    fetch[3].wait()
    for s in range(2):
        r.pack_t[s] = tough_ref[0, :, 0:2] if s == 0 else tough_ref[0, :, ny - 2 : ny]
    for sx in range(2):
        for sy in range(2):
            row = 0 if sy == 0 else ny - 1
            r.pack_tk[sx * 2 + sy] = tough_ref[0, 0 if sx == 0 else nx - 1, row : row + 1]
    last_one.start()

    tough_copies = []
    for k in range(1, sections):
        copy = pltpu.make_async_remote_copy(
            src_ref=tough_ref.at[0],
            dst_ref=r.tough_in.at[k - 1],
            send_sem=r.tough_send.at[k - 1],
            recv_sem=r.tough_recv.at[k - 1],
            device_id={"section": lax.rem(sec + sections - k, sections)},
            device_id_type=MESH,
        )
        copy.start()
        tough_copies.append(copy)

    inner = slice(OY, OY + ny)
    as_float = lambda v: v.astype(jnp.float32)

    def fill(x, carry):
        load = as_float(load_ref[x])
        clamp = as_float(clamp_ref[x])
        held[x + HX, inner] = load
        clamped[x + HX, inner] = clamp
        free[x + HX, inner] = 1.0 - jnp.maximum(clamp, load)
        crack_pad[x + HX, inner] = as_float(crack_ref[x])
        tough_pad[x + HX, inner] = tough_ref[0, x]
        return carry

    lax.fori_loop(0, nx, fill, 0, unroll=part(nx, 4))

    for copy in fetch[4:]:
        copy.wait()
    case = r.index_ref[0]
    vector = [r.table_ref[f, case] for f in range(3)]

    planes = slice(HX, HX + nx)

    def x_out(s, n):
        return slice(HX - n, HX) if s == 0 else slice(HX + nx, HX + nx + n)

    def y_out(s, n):
        return slice(OY - n, OY) if s == 0 else slice(OY + ny, OY + ny + n)

    early.received()
    for s in range(2):

        @pl.when(there["gx"][s])
        def _(s=s):
            held[x_out(s, 5), inner] = as_float(r.in_x[s, 0:5])
            crack_pad[x_out(s, 4), inner] = as_float(r.in_x[s, 5:9])

        @pl.when(there["gy"][s])
        def _(s=s):
            held[planes, y_out(s, 5)] = as_float(r.in_l[s, :, 0:5])
            clamped[planes, y_out(s, 3)] = as_float(r.in_l[s, :, 5:8])
            crack_pad[planes, y_out(s, 4)] = as_float(r.in_c[s])

    for sx in range(2):
        for sy in range(2):

            @pl.when(c_dev(sx, sy)[0])
            def _(sx=sx, sy=sy):
                for _, pad, deep, n, at in corner:
                    plane = HX - deep if sx == 0 else HX + nx - 1 + deep
                    pad[plane, y_out(sy, n)] = as_float(
                        r.in_k[sx * 2 + sy, at // 8, at % 8 : at % 8 + n]
                    )

    wide = up8(ny + 4)
    near = up8(ny + 2)
    deep = up8(ny + 8)

    def lanes(shape, lane):
        return lax.broadcasted_iota(jnp.int32, shape, 1) == lane

    def beside(v, edge, first, last):
        up = jnp.where(last, edge, pltpu.roll(v, nz - 1, 1))
        down = jnp.where(first, edge, pltpu.roll(v, 1, 1))
        return up, down

    def inside_rows(shape, above):
        row = lax.broadcasted_iota(jnp.int32, shape, 0) + (gy * ny - above)
        return jnp.logical_and(row >= 0, row < ny * ngy)

    def inside_plane(xp):
        plane = xp - HX + gx * nx
        return jnp.logical_and(plane >= 0, plane < nx * ngx)

    edge_stiff = 0.5 * (1.0 + stiff_floor)

    def elastic(at, first, last):
        k = at(stiff, 0, 0)
        sides = (
            (at(stiff, 1, 0), at(stiff, -1, 0)),
            (at(stiff, 0, 1), at(stiff, 0, -1)),
            beside(k, edge_stiff, first, last),
        )
        pairs = [s[0] + s[1] for s in sides]
        weights = pairs[0] + pairs[1] + pairs[2] + 6.0 * k
        faces = [(k + s[0], k + s[1]) for s in sides]
        fz = beside(at(flow, 0, 0), 0.0, first, last)
        grads = (
            at(flow, 1, 0) - at(flow, -1, 0),
            at(flow, 0, 1) - at(flow, 0, -1),
            fz[0] - fz[1],
        )
        return pairs, weights, faces, grads

    def laplace(at, ref, faces, weights, first, last):
        here = at(ref, 0, 0)
        uz = beside(here, 0.0, first, last)
        return here, (
            faces[0][0] * at(ref, 1, 0)
            + faces[0][1] * at(ref, -1, 0)
            + faces[1][0] * at(ref, 0, 1)
            + faces[1][1] * at(ref, 0, -1)
            + faces[2][0] * uz[0]
            + faces[2][1] * uz[1]
            - weights * here
        )

    def strain_energy(at, u, keep, first, last):
        grad = []
        for f in range(3):
            here = at(u.at[f], 0, 0)
            uz = beside(here, 0.0, first, last)
            grad.append(
                (
                    at(u.at[f], 1, 0) - at(u.at[f], -1, 0),
                    at(u.at[f], 0, 1) - at(u.at[f], 0, -1),
                    uz[0] - uz[1],
                )
            )
            keep(f, here)
        return 2.0 * spectral_energy(
            0.5 * grad[0][0],
            0.5 * grad[1][1],
            0.5 * grad[2][2],
            0.25 * (grad[0][1] + grad[1][0]),
            0.25 * (grad[0][2] + grad[2][0]),
            0.25 * (grad[1][2] + grad[2][1]),
        )

    def renew(at, d, energy, g, cracked, first, last):
        dz = beside(at(d, 0, 0), 0.0, first, last)
        around = at(d, 1, 0) + at(d, -1, 0) + at(d, 0, 1) + at(d, 0, -1) + dz[0] + dz[1]
        renewed = (energy + g * around) / (7.0 * g + energy)
        return jnp.where(cracked, 1.0, renewed)

    def add_up(rnd, total):
        r.sums[me, rnd : rnd + 1] = jnp.sum(total, axis=0, keepdims=True)

    def open_sweep():
        shape = (deep, nz)
        first, last = lanes(shape, 0), lanes(shape, nz - 1)
        row_inside = inside_rows(shape, 4)
        a = OY - 4

        def stiffen(xp, carry):
            half = 0.5 * (jnp.square(1.0 - crack_pad[xp, a : a + deep]) + stiff_floor)
            stiff[xp, a : a + deep] = half
            up, down = beside(held[xp, a : a + deep], 0.0, first, last)
            div = (
                vector[0] * (held[xp + 1, a : a + deep] - held[xp - 1, a : a + deep])
                + vector[1] * (held[xp, a + 1 : a + 1 + deep] - held[xp, a - 1 : a - 1 + deep])
                + vector[2] * (up - down)
            )
            flow[xp, a : a + deep] = jnp.where(
                jnp.logical_and(row_inside, inside_plane(xp)), half * div, 0.0
            )
            return carry

        lax.fori_loop(HX - 4, HX + nx + 4, stiffen, 0, unroll=part(nx + 8, 8))

        later.received()
        for s in range(2):

            @pl.when(there["gx"][s])
            def _(s=s):
                clamped[x_out(s, 3), inner] = as_float(r.in_x[s, 9:12])

        def move(xp, total):
            at = lambda ref, dx, dy: ref[xp + dx, a + dy : a + dy + deep]
            pairs, weights, faces, grads = elastic(at, first, last)
            load, spread = laplace(at, held, faces, weights, first, last)
            pin = at(clamped, 0, 0) + load > 0.5
            squares = None
            for f in range(3):
                res = vector[f] * spread + grads[f]
                moved = jnp.where(pin, 0.0, relax_weight * res / (weights + pairs[f]))
                state[1, f, xp, a : a + deep] = vector[f] * load + moved
                square = res * res
                squares = square if squares is None else squares + square
            return total + jnp.where(at(free, 0, 0) > 0.5, squares, 0.0)

        total = lax.fori_loop(
            HX - 3,
            HX + nx + 3,
            move,
            jnp.zeros(shape, jnp.float32),
            unroll=part(nx + 6, 11),
        )
        add_up(0, total)

        last_one.received()
        for s in range(2):

            @pl.when(there["gx"][s])
            def _(s=s):
                tough_pad[x_out(s, 2), inner] = r.in_tx[s]

            @pl.when(there["gy"][s])
            def _(s=s):
                tough_pad[planes, y_out(s, 2)] = r.in_ty[s]

        for sx in range(2):
            for sy in range(2):

                @pl.when(c_dev(sx, sy)[0])
                def _(sx=sx, sy=sy):
                    plane = HX - 1 if sx == 0 else HX + nx
                    tough_pad[plane, y_out(sy, 1)] = r.in_tk[sx * 2 + sy]

        def damage(xp, carry):
            at = lambda ref, dx, dy: ref[xp + dx, a + dy : a + dy + deep]
            energy = strain_energy(at, state.at[1], lambda f, v: None, first, last)
            renewed = renew(
                at,
                crack_pad,
                energy,
                at(tough_pad, 0, 0),
                at(crack_pad, 0, 0) > 0.5,
                first,
                last,
            )
            state[1, 3, xp, a : a + deep] = jnp.where(
                jnp.logical_and(row_inside, inside_plane(xp)), renewed, 0.0
            )
            return carry

        lax.fori_loop(HX - 2, HX + nx + 2, damage, 0, unroll=part(nx + 4, 5))

    def send_sums():
        for k, peer in enumerate(peers):
            pltpu.make_async_remote_copy(
                src_ref=r.sums.at[me],
                dst_ref=r.sums.at[me],
                send_sem=r.sum_send.at[k],
                recv_sem=r.sum_recv.at[me],
                device_id=peer,
                device_id_type=MESH,
            ).start()

    def sweep(rnd):
        p = rnd % 2
        q = 1 - p
        done = rnd == sections - 1
        tough = r.tough_in.at[rnd - 1]

        shape = (wide, nz)
        first, last = lanes(shape, 0), lanes(shape, nz - 1)
        row_inside = inside_rows(shape, 2)
        a = OY - 2

        def stiffen(xp, carry):
            half = 0.5 * (jnp.square(1.0 - state[p, 3, xp, a : a + wide]) + stiff_floor)
            stiff[xp, a : a + wide] = half
            up, down = beside(state[p, 2, xp, a : a + wide], 0.0, first, last)
            div = (
                (state[p, 0, xp + 1, a : a + wide] - state[p, 0, xp - 1, a : a + wide])
                + (state[p, 1, xp, a + 1 : a + 1 + wide] - state[p, 1, xp, a - 1 : a - 1 + wide])
                + (up - down)
            )
            flow[xp, a : a + wide] = jnp.where(
                jnp.logical_and(row_inside, inside_plane(xp)), half * div, 0.0
            )
            return carry

        lax.fori_loop(HX - 2, HX + nx + 2, stiffen, 0, unroll=part(nx + 4, 10))

        shape = (near, nz)
        first, last = lanes(shape, 0), lanes(shape, nz - 1)
        b = OY - 1

        def move(xp, total):
            at = lambda ref, dx, dy: ref[xp + dx, b + dy : b + dy + near]
            pairs, weights, faces, grads = elastic(at, first, last)
            load = at(held, 0, 0)
            pin = at(clamped, 0, 0) + load > 0.5
            squares = None
            for f in range(3):
                here, spread = laplace(at, state.at[p, f], faces, weights, first, last)
                res = spread + grads[f]
                moved = here + relax_weight * res / (weights + pairs[f])
                state[q, f, xp, b : b + near] = jnp.where(pin, load * vector[f], moved)
                square = res * res
                squares = square if squares is None else squares + square
            return total + jnp.where(at(free, 0, 0) > 0.5, squares, 0.0)

        total = lax.fori_loop(
            HX - 1, HX + nx + 1, move, jnp.zeros(shape, jnp.float32), unroll=part(nx + 2, 6)
        )
        add_up(rnd, total)
        par = rnd % 2
        mid = pl.ds(OY, ny)
        if done:
            send_sums()
        else:
            for f in range(3):
                r.pack_u[0, :, 2 * f : 2 * f + 2] = state[q, f, planes, OY : OY + 2]
                r.pack_u[1, :, 2 * f : 2 * f + 2] = state[q, f, planes, OY + ny - 2 : OY + ny]
            r.pack_u[0, :, 6:7] = state[q, 1, planes, OY + 2 : OY + 3]
            r.pack_u[1, :, 6:7] = state[q, 1, planes, OY + ny - 3 : OY + ny - 2]
            shift = Exchange(r.u_send, r.u_recv.at[par])
            for s in range(2):
                shift.add(
                    x_dev(s),
                    state.at[q, pl.ds(0, 3), pl.ds(HX if s == 0 else HX + nx - 2, 2), mid],
                    r.in_u_x.at[par, 1 - s],
                    r.in_u_x.at[par, s],
                    (1 - s),
                    s,
                )
                shift.add(
                    x_dev(s),
                    state.at[q, 0, HX + 2 if s == 0 else HX + nx - 3, mid],
                    r.in_u_x3.at[par, 1 - s],
                    r.in_u_x3.at[par, s],
                    2 + (1 - s),
                    2 + s,
                )
            for s in range(2):
                shift.add(
                    y_dev(s),
                    r.pack_u.at[s],
                    r.in_u_y.at[par, 1 - s],
                    r.in_u_y.at[par, s],
                    4 + (1 - s),
                    4 + s,
                )
            for sx in range(2):
                for sy in range(2):
                    shift.add(
                        c_dev(sx, sy),
                        r.pack_u.at[sy, pl.ds(0 if sx == 0 else nx - 2, 2)],
                        r.in_u_c.at[par, (1 - sx) * 2 + 1 - sy],
                        r.in_u_c.at[par, sx * 2 + sy],
                        6 + (1 - sx) * 2 + 1 - sy,
                        6 + sx * 2 + sy,
                    )
            shift.start()

        tough_copies[rnd - 1].wait_recv()

        shape = (ny, nz)
        first, last = lanes(shape, 0), lanes(shape, nz - 1)

        def damage(x, carry):
            xp = x + HX
            at = lambda ref, dx, dy: ref[xp + dx, OY + dy : OY + dy + ny]

            def keep(f, here):
                if done:
                    disp_refs[f][x] = here

            energy = strain_energy(at, state.at[q], keep, first, last)
            renewed = renew(
                at, state.at[p, 3], energy, tough[x], crack_ref[x] > 0, first, last
            )
            if done:
                r.dam_ref[x] = renewed
            else:
                state[q, 3, xp, inner] = renewed
            return carry

        lax.fori_loop(0, nx, damage, 0, unroll=part(nx, 8))
        if done:
            return

        r.pack_d[0] = state[q, 3, planes, OY : OY + 2]
        r.pack_d[1] = state[q, 3, planes, OY + ny - 2 : OY + ny]
        crack = Exchange(r.d_send, r.d_recv.at[par])
        for s in range(2):
            crack.add(
                x_dev(s),
                state.at[q, 3, pl.ds(HX if s == 0 else HX + nx - 2, 2), mid],
                r.in_d_x.at[par, 1 - s],
                r.in_d_x.at[par, s],
                1 - s,
                s,
            )
        for s in range(2):
            crack.add(
                y_dev(s),
                r.pack_d.at[s],
                r.in_d_y.at[par, 1 - s],
                r.in_d_y.at[par, s],
                2 + 1 - s,
                2 + s,
            )
        for sx in range(2):
            for sy in range(2):
                crack.add(
                    c_dev(sx, sy),
                    r.pack_d.at[sy, pl.ds(0 if sx == 0 else nx - 1, 1)],
                    r.in_d_c.at[par, (1 - sx) * 2 + 1 - sy],
                    r.in_d_c.at[par, sx * 2 + sy],
                    4 + (1 - sx) * 2 + 1 - sy,
                    4 + sx * 2 + sy,
                )
        crack.start()
        shift.finish()
        third_x = (HX - 3, HX + nx + 2)
        third_y = (slice(OY - 3, OY - 2), slice(OY + ny + 2, OY + ny + 3))
        for s in range(2):

            @pl.when(there["gx"][s])
            def _(s=s):
                state[q, 0:3, x_out(s, 2), inner] = r.in_u_x[par, s]
                state[q, 0, third_x[s], inner] = r.in_u_x3[par, s]

            @pl.when(there["gy"][s])
            def _(s=s):
                for f in range(3):
                    state[q, f, planes, y_out(s, 2)] = r.in_u_y[par, s, :, 2 * f : 2 * f + 2]
                state[q, 1, planes, third_y[s]] = r.in_u_y[par, s, :, 6:7]

        for sx in range(2):
            for sy in range(2):

                @pl.when(c_dev(sx, sy)[0])
                def _(sx=sx, sy=sy):
                    for f in range(3):
                        state[q, f, x_out(sx, 2), y_out(sy, 2)] = r.in_u_c[
                            par, sx * 2 + sy, :, 2 * f : 2 * f + 2
                        ]

        crack.finish()
        for s in range(2):

            @pl.when(there["gx"][s])
            def _(s=s):
                state[q, 3, x_out(s, 2), inner] = r.in_d_x[par, s]

            @pl.when(there["gy"][s])
            def _(s=s):
                state[q, 3, planes, y_out(s, 2)] = r.in_d_y[par, s]

        for sx in range(2):
            for sy in range(2):

                @pl.when(c_dev(sx, sy)[0])
                def _(sx=sx, sy=sy):
                    state[q, 3, x_out(sx, 1), y_out(sy, 2)] = r.in_d_c[par, sx * 2 + sy]

    open_sweep()
    if sections == 1:
        send_sums()
    for rnd in range(1, sections):
        sweep(rnd)

    cells = 3.0 * nx * ngx * ny * ngy * nz
    early.sent()
    later.sent()
    last_one.sent()
    for copy in tough_copies:
        copy.wait_send()
    for k in range(1, group):
        other = lax.rem(me + k, group)
        pltpu.make_async_remote_copy(
            src_ref=r.sums.at[me],
            dst_ref=r.sums.at[other],
            send_sem=r.sum_send.at[k - 1],
            recv_sem=r.sum_recv.at[other],
            device_id=peers[k - 1],
            device_id_type=MESH,
        ).wait()
    total = r.sums[0]
    for k in range(1, group):
        total = total + r.sums[k]
    entries = jnp.sqrt(jnp.sum(total, axis=1, keepdims=True) / cells)
    column = lax.broadcasted_iota(jnp.int32, (1, sections), 1)
    norms = jnp.zeros((1, sections), jnp.float32)
    for rnd in range(sections):
        norms = jnp.where(
            column == lax.rem(sec + rnd, sections), entries[rnd : rnd + 1], norms
        )
    r.norm_ref[...] = norms


def put_out(
    first_ref, second_ref, third_ref, dam_ref, norm_ref, disp_hbm, dam_hbm, norm_out, sems
):
    copies = [
        pltpu.make_async_copy(ref, disp_hbm.at[0, f], sems.at[f])
        for f, ref in enumerate((first_ref, second_ref, third_ref))
    ]
    copies.append(pltpu.make_async_copy(dam_ref, dam_hbm.at[0], sems.at[3]))
    for copy in copies:
        copy.start()
    norm_out[...] = norm_ref[...]
    for copy in copies:
        copy.wait()


def on_device(sizes, load_index, load_table, toughness, clamp_mask, load_mask, crack_mask):
    sections, ngx, ngy = sizes
    nx, ny, nz = clamp_mask.shape
    assert load_index.shape == (1,)
    group = ngx * ngy
    f32 = jnp.float32
    padded = (nx + 2 * HX, ny + 2 * OY, nz)
    vmem = pltpu.VMEM
    dma = pltpu.SemaphoreType.DMA
    later = max(sections - 1, 1)
    more = sections > 2
    scratch = {
        "index_ref": pltpu.SMEM(load_index.shape, jnp.int32),
        "table_ref": pltpu.SMEM(load_table.shape[::-1], f32),
        "tough_ref": vmem((1, nx, ny, nz), f32),
        "clamp_ref": vmem((nx, ny, nz), jnp.int32),
        "load_ref": vmem((nx, ny, nz), jnp.int32),
        "crack_ref": vmem((nx, ny, nz), jnp.int32),
        "local": dma((6,)),
        "state": vmem((2, 4) + padded, f32),
        "stiff": vmem(padded, f32),
        "flow": vmem(padded, f32),
        "held": vmem(padded, f32),
        "clamped": vmem(padded, f32),
        "free": vmem(padded, f32),
        "tough_pad": vmem(padded, f32),
        "crack_pad": vmem(padded, f32),
        "tough_in": vmem((later, nx, ny, nz), f32),
        "pack_l": vmem((2, nx, 8, nz), jnp.int32),
        "pack_c": vmem((2, nx, 4, nz), jnp.int32),
        "pack_t": vmem((2, nx, 2, nz), f32),
        "pack_k": vmem((4, 3, 8, nz), jnp.int32),
        "pack_tk": vmem((4, 1, nz), f32),
        "in_x": vmem((2, 12, ny, nz), jnp.int32),
        "in_tx": vmem((2, 2, ny, nz), f32),
        "in_l": vmem((2, nx, 8, nz), jnp.int32),
        "in_c": vmem((2, nx, 4, nz), jnp.int32),
        "in_ty": vmem((2, nx, 2, nz), f32),
        "in_k": vmem((4, 3, 8, nz), jnp.int32),
        "in_tk": vmem((4, 1, nz), f32),
        "sums": vmem((group, sections, nz), f32),
        "early_send": dma((12,)),
        "early_recv": dma((12,)),
        "later_send": dma((2,)),
        "later_recv": dma((2,)),
        "last_send": dma((8,)),
        "last_recv": dma((8,)),
        "tough_send": dma((later,)),
        "tough_recv": dma((later,)),
        "sum_send": dma((max(group - 1, 1),)),
        "sum_recv": dma((group,)),
    }
    if more:
        scratch |= {
            "pack_u": vmem((2, nx, 8, nz), f32),
            "pack_d": vmem((2, nx, 2, nz), f32),
            "in_u_x": vmem((2, 2, 3, 2, ny, nz), f32),
            "in_u_x3": vmem((2, 2, ny, nz), f32),
            "in_u_y": vmem((2, 2, nx, 8, nz), f32),
            "in_u_c": vmem((2, 4, 2, 8, nz), f32),
            "in_d_x": vmem((2, 2, 2, ny, nz), f32),
            "in_d_y": vmem((2, 2, nx, 2, nz), f32),
            "in_d_c": vmem((2, 4, 1, 2, nz), f32),
            "u_send": dma((10,)),
            "u_recv": dma((2, 10)),
            "d_send": dma((8,)),
            "d_recv": dma((2, 8)),
        }
    ins = ("index_hbm", "table_hbm", "tough_hbm", "clamp_hbm", "load_hbm", "crack_hbm")
    outs = ("first_ref", "second_ref", "third_ref", "dam_ref", "norm_ref")
    names = (*ins, *outs, *scratch)
    block = pl.BlockSpec(memory_space=pltpu.VMEM)
    away = pl.BlockSpec(memory_space=pltpu.HBM)
    results = pl.pallas_call(
        functools.partial(kernel, (sections, ngx, ngy, nx, ny, nz), names),
        out_shape=(
            *[jax.ShapeDtypeStruct((nx, ny, nz), f32)] * 4,
            jax.ShapeDtypeStruct((1, sections), f32),
        ),
        in_specs=[away] * 6,
        out_specs=(block,) * 5,
        scratch_shapes=list(scratch.values()),
        compiler_params=pltpu.CompilerParams(
            collective_id=0, has_side_effects=True, vmem_limit_bytes=56_020_000
        ),
    )(load_index, load_table.T, toughness, clamp_mask, load_mask, crack_mask)
    return pl.pallas_call(
        put_out,
        out_shape=(
            jax.ShapeDtypeStruct((1, 3, nx, ny, nz), f32),
            jax.ShapeDtypeStruct((1, nx, ny, nz), f32),
            jax.ShapeDtypeStruct((1, sections), f32),
        ),
        in_specs=[block] * 5,
        out_specs=(away, away, block),
        scratch_shapes=[dma((4,))],
        compiler_params=pltpu.CompilerParams(vmem_limit_bytes=1024 * 1024),
    )(*results)


def solution(mesh):
    in_specs = (
        P("section"),
        P(),
        P("section", "gx", "gy", None),
        P("gx", "gy", None),
        P("gx", "gy", None),
        P("gx", "gy", None),
    )
    out_specs = (
        P("section", None, "gx", "gy", None),
        P("section", "gx", "gy", None),
        P("section", None),
    )
    sizes = tuple(mesh.shape[name] for name in ("section", "gx", "gy"))
    return jax.shard_map(
        functools.partial(on_device, sizes),
        mesh=mesh,
        in_specs=in_specs,
        out_specs=out_specs,
        check_vma=False,
    )
```

time: 23.9 us -> 20.9 us (0.87)
  Pallas kernels: 22.4 us -> 19.4 us
    pallas_call x1, Pallas kernels: 21.1 us -> 18.1 us  [on_device(): pl.pallas_call(functools.partial(kernel, (sections, ngx, ngy, nx, ny, nz)...]
where the time goes in v2:
time: 20.9 us; the launch traced here: 20.7 us
  Pallas kernels  19.4 us (93%)
  between operations  1.31 us (6%)
    pallas_call x1, Pallas kernels, on_device(): pl.pallas_call(functools.partial(kernel, (sections, ngx, ngy, nx, ny, nz)...  18.1 us
    pallas_call x1, Pallas kernels, on_device(): pl.pallas_call(put_out, out_shape=(jax.ShapeDtypeStruct((1, 3, nx, ny, nz...  1.33 us

profile of v2, /device:TPU:0, one launch (start us, length us, event | category | flops | bytes accessed | tf_op | source)
XLA Modules:
  0.0 20.7 jit_solution(1602309134568137145)
XLA Ops:
  0.6 0.0 copy-start
  1.3 0.0 copy-done
  1.3 18.1 %shard_map.85 = (f32[16,16,128]{2,1,0:T(8,128)S(1)}, f32[16,16,128]{2,1,0:T(8,128)S(1)}, f32[16,16,128]{2,1,0:T(8,128)S(1)}, f32[16,16,128]{2,1,0:T(8,128)S(1)}, f32[1,2]{1,0:T(1,128)S(1)}) custom-call(s32[1]{0:T(128)S(6)} %copy.9.refs_0_, f32[3,64]{1,0:T(4,128)S(1)} %bitcast.1, f32[1,16,16,128]{3,2,1,0:T(8,128)} %refs_2_.1, s32[16,16,128]{2,1,0:T(8,128)} %refs_3_.1, ...), custom_call_target="tpu_custom_call" | custom-call | tf_op jit(solution)/shard_map/pallas_call | solution.py:862
  19.4 1.3 %shard_map.86 = (f32[1,3,16,16,128]{4,3,2,1,0:T(8,128)}, f32[1,16,16,128]{3,2,1,0:T(8,128)}, f32[1,2]{1,0:T(1,128)}) custom-call(f32[16,16,128]{2,1,0:T(8,128)S(1)} %get-tuple-element.8.first_ref, f32[16,16,128]{2,1,0:T(8,128)S(1)} %get-tuple-element.9.second_ref, f32[16,16,128]{2,1,0:T(8,128)S(1)} %get-tuple-element.10.third_ref, ...), custom_call_target="tpu_custom_call" | custom-call | tf_op jit(solution)/shard_map/pallas_call | solution.py:875
Async XLA Ops:
  0.6 0.7 %copy-start = (f32[64,3]{0,1:T(4,128)S(1)}, f32[64,3]{0,1:T(4,128)}, u32[]{:S(2)}) copy-start(f32[64,3]{0,1:T(4,128)} %param.7) | copy-start | bytes 2308

commit v3 on v2

--- a/solution.py
+++ b/solution.py
@@ -168,8 +168,8 @@
             )
             self.items.append((cond, copy, back))
 
-        def start(self):
-            for cond, copy, _ in self.items:
+        def start(self, begin=0, end=None):
+            for cond, copy, _ in self.items[begin:end]:
                 pl.when(cond)(copy.start)
 
         def finish(self):
@@ -233,6 +233,7 @@
 
     pl.semaphore_wait(barrier, group - 1 + sections - 1)
 
+    beside_y = Exchange(r.y_send, r.y_recv)
     early = Exchange(r.early_send, r.early_recv)
     later = Exchange(r.later_send, r.later_recv)
     last_one = Exchange(r.last_send, r.last_recv)
@@ -252,12 +253,12 @@
                 slot + s,
             )
     for s in range(2):
-        for ex, pack, buf, slot in (
-            (early, r.pack_l, r.in_l, 4),
-            (early, r.pack_c, r.in_c, 6),
-            (last_one, r.pack_t, r.in_ty, 2),
+        for pack, buf, slot in (
+            (r.pack_l, r.in_l, 0),
+            (r.pack_c, r.in_c, 2),
+            (r.pack_t, r.in_ty, 4),
         ):
-            ex.add(
+            beside_y.add(
                 y_dev(s), pack.at[s], buf.at[1 - s], buf.at[s], slot + 1 - s, slot + s
             )
     for sx in range(2):
@@ -265,15 +266,13 @@
             here, away = sx * 2 + sy, (1 - sx) * 2 + 1 - sy
             early.add(
                 c_dev(sx, sy), r.pack_k.at[here], r.in_k.at[away], r.in_k.at[here],
-                8 + away, 8 + here,
+                4 + away, 4 + here,
             )
             last_one.add(
                 c_dev(sx, sy), r.pack_tk.at[here], r.in_tk.at[away], r.in_tk.at[here],
-                4 + away, 4 + here,
-            )
-    early.start()
-    later.start()
-
+                2 + away, 2 + here,
+            )
+    early.start(0, 4)
     fetch[3].wait()
     for s in range(2):
         r.pack_t[s] = tough_ref[0, :, 0:2] if s == 0 else tough_ref[0, :, ny - 2 : ny]
@@ -281,6 +280,9 @@
         for sy in range(2):
             row = 0 if sy == 0 else ny - 1
             r.pack_tk[sx * 2 + sy] = tough_ref[0, 0 if sx == 0 else nx - 1, row : row + 1]
+    beside_y.start()
+    early.start(4)
+    later.start()
     last_one.start()
 
     tough_copies = []
@@ -324,33 +326,62 @@
     def y_out(s, n):
         return slice(OY - n, OY) if s == 0 else slice(OY + ny, OY + ny + n)
 
-    early.received()
-    for s in range(2):
-
-        @pl.when(there["gx"][s])
-        def _(s=s):
-            held[x_out(s, 5), inner] = as_float(r.in_x[s, 0:5])
-            crack_pad[x_out(s, 4), inner] = as_float(r.in_x[s, 5:9])
-
-        @pl.when(there["gy"][s])
-        def _(s=s):
-            held[planes, y_out(s, 5)] = as_float(r.in_l[s, :, 0:5])
-            clamped[planes, y_out(s, 3)] = as_float(r.in_l[s, :, 5:8])
-            crack_pad[planes, y_out(s, 4)] = as_float(r.in_c[s])
-
-    for sx in range(2):
-        for sy in range(2):
-
-            @pl.when(c_dev(sx, sy)[0])
-            def _(sx=sx, sy=sy):
-                for _, pad, deep, n, at in corner:
-                    plane = HX - deep if sx == 0 else HX + nx - 1 + deep
-                    pad[plane, y_out(sy, n)] = as_float(
-                        r.in_k[sx * 2 + sy, at // 8, at % 8 : at % 8 + n]
-                    )
+    def unpack_y():
+        beside_y.received()
+        for s in range(2):
+
+            @pl.when(there["gy"][s])
+            def _(s=s):
+                held[planes, y_out(s, 5)] = as_float(r.in_l[s, :, 0:5])
+                clamped[planes, y_out(s, 3)] = as_float(r.in_l[s, :, 5:8])
+                crack_pad[planes, y_out(s, 4)] = as_float(r.in_c[s])
+                tough_pad[planes, y_out(s, 2)] = r.in_ty[s]
+
+    def unpack_x():
+        early.received()
+        for s in range(2):
+
+            @pl.when(there["gx"][s])
+            def _(s=s):
+                held[x_out(s, 5), inner] = as_float(r.in_x[s, 0:5])
+                crack_pad[x_out(s, 4), inner] = as_float(r.in_x[s, 5:9])
+
+        for sx in range(2):
+            for sy in range(2):
+
+                @pl.when(c_dev(sx, sy)[0])
+                def _(sx=sx, sy=sy):
+                    for _, pad, deep, n, at in corner:
+                        plane = HX - deep if sx == 0 else HX + nx - 1 + deep
+                        pad[plane, y_out(sy, n)] = as_float(
+                            r.in_k[sx * 2 + sy, at // 8, at % 8 : at % 8 + n]
+                        )
+
+    def unpack_clamp():
+        later.received()
+        for s in range(2):
+
+            @pl.when(there["gx"][s])
+            def _(s=s):
+                clamped[x_out(s, 3), inner] = as_float(r.in_x[s, 9:12])
+
+    def unpack_tough():
+        last_one.received()
+        for s in range(2):
+
+            @pl.when(there["gx"][s])
+            def _(s=s):
+                tough_pad[x_out(s, 2), inner] = r.in_tx[s]
+
+        for sx in range(2):
+            for sy in range(2):
+
+                @pl.when(c_dev(sx, sy)[0])
+                def _(sx=sx, sy=sy):
+                    plane = HX - 1 if sx == 0 else HX + nx
+                    tough_pad[plane, y_out(sy, 1)] = r.in_tk[sx * 2 + sy]
 
     wide = up8(ny + 4)
-    near = up8(ny + 2)
     deep = up8(ny + 8)
 
     def lanes(shape, lane):
@@ -453,15 +484,6 @@
             )
             return carry
 
-        lax.fori_loop(HX - 4, HX + nx + 4, stiffen, 0, unroll=part(nx + 8, 8))
-
-        later.received()
-        for s in range(2):
-
-            @pl.when(there["gx"][s])
-            def _(s=s):
-                clamped[x_out(s, 3), inner] = as_float(r.in_x[s, 9:12])
-
         def move(xp, total):
             at = lambda ref, dx, dy: ref[xp + dx, a + dy : a + dy + deep]
             pairs, weights, faces, grads = elastic(at, first, last)
@@ -476,34 +498,6 @@
                 squares = square if squares is None else squares + square
             return total + jnp.where(at(free, 0, 0) > 0.5, squares, 0.0)
 
-        total = lax.fori_loop(
-            HX - 3,
-            HX + nx + 3,
-            move,
-            jnp.zeros(shape, jnp.float32),
-            unroll=part(nx + 6, 11),
-        )
-        add_up(0, total)
-
-        last_one.received()
-        for s in range(2):
-
-            @pl.when(there["gx"][s])
-            def _(s=s):
-                tough_pad[x_out(s, 2), inner] = r.in_tx[s]
-
-            @pl.when(there["gy"][s])
-            def _(s=s):
-                tough_pad[planes, y_out(s, 2)] = r.in_ty[s]
-
-        for sx in range(2):
-            for sy in range(2):
-
-                @pl.when(c_dev(sx, sy)[0])
-                def _(sx=sx, sy=sy):
-                    plane = HX - 1 if sx == 0 else HX + nx
-                    tough_pad[plane, y_out(sy, 1)] = r.in_tk[sx * 2 + sy]
-
         def damage(xp, carry):
             at = lambda ref, dx, dy: ref[xp + dx, a + dy : a + dy + deep]
             energy = strain_energy(at, state.at[1], lambda f, v: None, first, last)
@@ -521,7 +515,28 @@
             )
             return carry
 
-        lax.fori_loop(HX - 2, HX + nx + 2, damage, 0, unroll=part(nx + 4, 5))
+        def inward(skip, body, carry, most):
+            n = nx - 2 * skip
+            return lax.fori_loop(HX + skip, HX + nx - skip, body, carry, unroll=part(n, most))
+
+        def outward(far, body, carry):
+            def both(i, carry):
+                carry = body(HX - far + i, carry)
+                return body(HX + nx + far - 5 + i, carry)
+
+            return lax.fori_loop(0, 5, both, carry, unroll=True)
+
+        unpack_y()
+        inward(1, stiffen, 0, 14)
+        total = inward(2, move, jnp.zeros(shape, jnp.float32), 12)
+        inward(3, damage, 0, 5)
+        unpack_x()
+        outward(4, stiffen, 0)
+        unpack_clamp()
+        total = outward(3, move, total)
+        add_up(0, total)
+        unpack_tough()
+        outward(2, damage, 0)
 
     def send_sums():
         for k, peer in enumerate(peers):
@@ -561,34 +576,47 @@
 
         lax.fori_loop(HX - 2, HX + nx + 2, stiffen, 0, unroll=part(nx + 4, 10))
 
-        shape = (near, nz)
-        first, last = lanes(shape, 0), lanes(shape, nz - 1)
-        b = OY - 1
-
-        def move(xp, total):
-            at = lambda ref, dx, dy: ref[xp + dx, b + dy : b + dy + near]
-            pairs, weights, faces, grads = elastic(at, first, last)
-            load = at(held, 0, 0)
-            pin = at(clamped, 0, 0) + load > 0.5
-            squares = None
-            for f in range(3):
-                here, spread = laplace(at, state.at[p, f], faces, weights, first, last)
-                res = spread + grads[f]
-                moved = here + relax_weight * res / (weights + pairs[f])
-                state[q, f, xp, b : b + near] = jnp.where(pin, load * vector[f], moved)
-                square = res * res
-                squares = square if squares is None else squares + square
-            return total + jnp.where(at(free, 0, 0) > 0.5, squares, 0.0)
+        def mover(b, n):
+            shape = (n, nz)
+            first, last = lanes(shape, 0), lanes(shape, nz - 1)
+
+            def move(xp, total):
+                at = lambda ref, dx, dy: ref[xp + dx, b + dy : b + dy + n]
+                pairs, weights, faces, grads = elastic(at, first, last)
+                load = at(held, 0, 0)
+                pin = at(clamped, 0, 0) + load > 0.5
+                squares = None
+                for f in range(3):
+                    here, spread = laplace(at, state.at[p, f], faces, weights, first, last)
+                    res = spread + grads[f]
+                    moved = here + relax_weight * res / (weights + pairs[f])
+                    state[q, f, xp, b : b + n] = jnp.where(pin, load * vector[f], moved)
+                    square = res * res
+                    squares = square if squares is None else squares + square
+                return total + jnp.where(pin, 0.0, squares)
+
+            return move
 
         total = lax.fori_loop(
-            HX - 1, HX + nx + 1, move, jnp.zeros(shape, jnp.float32), unroll=part(nx + 2, 6)
+            HX, HX + nx, mover(OY, ny), jnp.zeros((ny, nz), jnp.float32), unroll=part(nx, 8)
         )
         add_up(rnd, total)
+        if done:
+            send_sums()
+        none = jnp.zeros((8, nz), jnp.float32)
+
+        def edges(xp, carry):
+            mover(OY - 4, 8)(xp, none)
+            mover(OY + ny - 3, 8)(xp, none)
+            return carry
+
+        lax.fori_loop(HX, HX + nx, edges, 0, unroll=part(nx, 8))
+        ends = mover(OY, ny)
+        ends(HX - 1, jnp.zeros((ny, nz), jnp.float32))
+        ends(HX + nx, jnp.zeros((ny, nz), jnp.float32))
         par = rnd % 2
         mid = pl.ds(OY, ny)
-        if done:
-            send_sums()
-        else:
+        if not done:
             for f in range(3):
                 r.pack_u[0, :, 2 * f : 2 * f + 2] = state[q, f, planes, OY : OY + 2]
                 r.pack_u[1, :, 2 * f : 2 * f + 2] = state[q, f, planes, OY + ny - 2 : OY + ny]
@@ -743,6 +771,7 @@
         sweep(rnd)
 
     cells = 3.0 * nx * ngx * ny * ngy * nz
+    beside_y.sent()
     early.sent()
     later.sent()
     last_one.sent()
@@ -827,12 +856,14 @@
         "in_k": vmem((4, 3, 8, nz), jnp.int32),
         "in_tk": vmem((4, 1, nz), f32),
         "sums": vmem((group, sections, nz), f32),
-        "early_send": dma((12,)),
-        "early_recv": dma((12,)),
+        "y_send": dma((6,)),
+        "y_recv": dma((6,)),
+        "early_send": dma((8,)),
+        "early_recv": dma((8,)),
         "later_send": dma((2,)),
         "later_recv": dma((2,)),
-        "last_send": dma((8,)),
-        "last_recv": dma((8,)),
+        "last_send": dma((6,)),
+        "last_recv": dma((6,)),
         "tough_send": dma((later,)),
         "tough_recv": dma((later,)),
         "sum_send": dma((max(group - 1, 1),)),
@@ -871,7 +902,7 @@
         compiler_params=pltpu.CompilerParams(
             collective_id=0, has_side_effects=True, vmem_limit_bytes=56_020_000
         ),
-    )(load_index, load_table.T, toughness, clamp_mask, load_mask, crack_mask)
+    )(load_index, pltpu.with_memory_space_constraint(load_table.T, pltpu.HBM), toughness, clamp_mask, load_mask, crack_mask)
     return pl.pallas_call(
         put_out,
         out_shape=(

time: 20.9 us -> 19.3 us (0.923)
  Pallas kernels: 19.4 us -> 17.8 us
    pallas_call x1, Pallas kernels: 18.1 us -> 16.5 us  [on_device(): pl.pallas_call(functools.partial(kernel, (sections, ngx, ngy, nx, ny, nz)...]
where the time goes in v3:
time: 19.3 us; the launch traced here: 19.1 us
  Pallas kernels  17.8 us (92%)
  between operations  1.28 us (7%)
    pallas_call x1, Pallas kernels, on_device(): pl.pallas_call(functools.partial(kernel, (sections, ngx, ngy, nx, ny, nz)...  16.5 us
    pallas_call x1, Pallas kernels, on_device(): pl.pallas_call(put_out, out_shape=(jax.ShapeDtypeStruct((1, 3, nx, ny, nz...  1.33 us

profile of v3, /device:TPU:0, one launch (start us, length us, event | category | flops | bytes accessed | tf_op | source)
XLA Modules:
  0.0 19.1 jit_solution(3050193282515787273)
XLA Ops:
  1.3 16.5 %shard_map.85 = (f32[16,16,128]{2,1,0:T(8,128)S(1)}, f32[16,16,128]{2,1,0:T(8,128)S(1)}, f32[16,16,128]{2,1,0:T(8,128)S(1)}, f32[16,16,128]{2,1,0:T(8,128)S(1)}, f32[1,2]{1,0:T(1,128)S(1)}) custom-call(s32[1]{0:T(128)S(6)} %copy.9.refs_0_, f32[3,64]{1,0:T(4,128)} %bitcast.1, f32[1,16,16,128]{3,2,1,0:T(8,128)} %refs_2_.1, s32[16,16,128]{2,1,0:T(8,128)} %refs_3_.1, ...), custom_call_target="tpu_custom_call" | custom-call | tf_op jit(solution)/shard_map/pallas_call | solution.py:893
  17.8 1.3 %shard_map.86 = (f32[1,3,16,16,128]{4,3,2,1,0:T(8,128)}, f32[1,16,16,128]{3,2,1,0:T(8,128)}, f32[1,2]{1,0:T(1,128)}) custom-call(f32[16,16,128]{2,1,0:T(8,128)S(1)} %get-tuple-element.8.first_ref, f32[16,16,128]{2,1,0:T(8,128)S(1)} %get-tuple-element.9.second_ref, f32[16,16,128]{2,1,0:T(8,128)S(1)} %get-tuple-element.10.third_ref, ...), custom_call_target="tpu_custom_call" | custom-call | tf_op jit(solution)/shard_map/pallas_call | solution.py:906

commit v4 on v3

--- a/solution.py
+++ b/solution.py
@@ -91,10 +91,23 @@
     gy = lax.axis_index("gy")
     group = ngx * ngy
     me = gx * ngy + gy
+    ring = lambda k, n: min(k, n - k)
+    offsets = [(i, j) for i in range(ngx) for j in range(ngy) if i or j]
+    offsets.sort(key=lambda o: (ring(o[0], ngx) + ring(o[1], ngy), o))
     peers = []
-    for k in range(1, group):
-        other = lax.rem(me + k, group)
-        peers.append({"gx": other // ngy, "gy": lax.rem(other, ngy)})
+    for i, j in offsets:
+        peers.append({"gx": lax.rem(gx + i, ngx), "gy": lax.rem(gy + j, ngy)})
+
+    barrier = pltpu.get_barrier_semaphore()
+    for peer in peers:
+        pl.semaphore_signal(barrier, inc=1, device_id=peer, device_id_type=MESH)
+    for k in range(1, sections):
+        pl.semaphore_signal(
+            barrier,
+            inc=1,
+            device_id={"section": lax.rem(sec + k, sections)},
+            device_id_type=MESH,
+        )
 
     fetch = [
         pltpu.make_async_copy(src, dst, local.at[n])
@@ -112,17 +125,6 @@
     for copy in fetch:
         copy.start()
 
-    barrier = pltpu.get_barrier_semaphore()
-    for peer in peers:
-        pl.semaphore_signal(barrier, inc=1, device_id=peer, device_id_type=MESH)
-    for k in range(1, sections):
-        pl.semaphore_signal(
-            barrier,
-            inc=1,
-            device_id={"section": lax.rem(sec + k, sections)},
-            device_id_type=MESH,
-        )
-
     there = {
         "gx": (gx > 0, gx < ngx - 1),
         "gy": (gy > 0, gy < ngy - 1),
@@ -180,8 +182,8 @@
                     back.wait_recv()
                     copy.wait_send()
 
-        def received(self):
-            for cond, _, back in self.items:
+        def received(self, begin=0, end=None):
+            for cond, _, back in self.items[begin:end]:
                 pl.when(cond)(back.wait_recv)
 
         def sent(self):
@@ -210,9 +212,10 @@
 
     for s in range(2):
         side = lambda n, s=s: slice(0, n) if s == 0 else slice(ny - n, ny)
-        r.pack_l[s, :, 0:5] = load_ref[:, side(5)]
-        r.pack_l[s, :, 5:8] = clamp_ref[:, side(3)]
         r.pack_c[s] = crack_ref[:, side(4)]
+        for x in range(nx):
+            r.pack_l[s, 5 * x : 5 * x + 5] = load_ref[x, side(5)]
+            r.pack_f[s, 3 * x : 3 * x + 3] = clamp_ref[x, side(3)]
     corner = (
         (load_ref, held, 1, 4, 0),
         (load_ref, held, 2, 3, 4),
@@ -229,7 +232,8 @@
             for ref, _, deep, n, at in corner:
                 plane = deep - 1 if sx == 0 else nx - deep
                 first = 0 if sy == 0 else ny - n
-                r.pack_k[sx * 2 + sy, at // 8, at % 8 : at % 8 + n] = ref[plane, first : first + n]
+                pack, at = (r.pack_k, at) if at < 16 else (r.pack_kf, at - 16)
+                pack[sx * 2 + sy, at : at + n] = ref[plane, first : first + n]
 
     pl.semaphore_wait(barrier, group - 1 + sections - 1)
 
@@ -252,12 +256,14 @@
                 slot + 1 - s,
                 slot + s,
             )
-    for s in range(2):
+    for n in range(8):
+        s = n % 2
         for pack, buf, slot in (
-            (r.pack_l, r.in_l, 0),
-            (r.pack_c, r.in_c, 2),
-            (r.pack_t, r.in_ty, 4),
-        ):
+            (r.pack_c, r.in_c, 0),
+            (r.pack_l, r.in_l, 2),
+            (r.pack_f, r.in_f, 4),
+            (r.pack_t, r.in_ty, 6),
+        )[n // 2 : n // 2 + 1]:
             beside_y.add(
                 y_dev(s), pack.at[s], buf.at[1 - s], buf.at[s], slot + 1 - s, slot + s
             )
@@ -268,11 +274,16 @@
                 c_dev(sx, sy), r.pack_k.at[here], r.in_k.at[away], r.in_k.at[here],
                 4 + away, 4 + here,
             )
+            later.add(
+                c_dev(sx, sy), r.pack_kf.at[here], r.in_kf.at[away], r.in_kf.at[here],
+                2 + away, 2 + here,
+            )
             last_one.add(
                 c_dev(sx, sy), r.pack_tk.at[here], r.in_tk.at[away], r.in_tk.at[here],
                 2 + away, 2 + here,
             )
     early.start(0, 4)
+    beside_y.start(0, 6)
     fetch[3].wait()
     for s in range(2):
         r.pack_t[s] = tough_ref[0, :, 0:2] if s == 0 else tough_ref[0, :, ny - 2 : ny]
@@ -280,7 +291,7 @@
         for sy in range(2):
             row = 0 if sy == 0 else ny - 1
             r.pack_tk[sx * 2 + sy] = tough_ref[0, 0 if sx == 0 else nx - 1, row : row + 1]
-    beside_y.start()
+    beside_y.start(6)
     early.start(4)
     later.start()
     last_one.start()
@@ -327,14 +338,30 @@
         return slice(OY - n, OY) if s == 0 else slice(OY + ny, OY + ny + n)
 
     def unpack_y():
-        beside_y.received()
+        beside_y.received(0, 4)
         for s in range(2):
 
             @pl.when(there["gy"][s])
             def _(s=s):
-                held[planes, y_out(s, 5)] = as_float(r.in_l[s, :, 0:5])
-                clamped[planes, y_out(s, 3)] = as_float(r.in_l[s, :, 5:8])
                 crack_pad[planes, y_out(s, 4)] = as_float(r.in_c[s])
+                for x in range(nx):
+                    held[HX + x, y_out(s, 5)] = as_float(r.in_l[s, 5 * x : 5 * x + 5])
+
+    def unpack_y_clamp():
+        beside_y.received(4, 6)
+        for s in range(2):
+
+            @pl.when(there["gy"][s])
+            def _(s=s):
+                for x in range(nx):
+                    clamped[HX + x, y_out(s, 3)] = as_float(r.in_f[s, 3 * x : 3 * x + 3])
+
+    def unpack_y_tough():
+        beside_y.received(6)
+        for s in range(2):
+
+            @pl.when(there["gy"][s])
+            def _(s=s):
                 tough_pad[planes, y_out(s, 2)] = r.in_ty[s]
 
     def unpack_x():
@@ -351,11 +378,9 @@
 
                 @pl.when(c_dev(sx, sy)[0])
                 def _(sx=sx, sy=sy):
-                    for _, pad, deep, n, at in corner:
+                    for _, pad, deep, n, at in corner[:-2]:
                         plane = HX - deep if sx == 0 else HX + nx - 1 + deep
-                        pad[plane, y_out(sy, n)] = as_float(
-                            r.in_k[sx * 2 + sy, at // 8, at % 8 : at % 8 + n]
-                        )
+                        pad[plane, y_out(sy, n)] = as_float(r.in_k[sx * 2 + sy, at : at + n])
 
     def unpack_clamp():
         later.received()
@@ -364,6 +389,16 @@
             @pl.when(there["gx"][s])
             def _(s=s):
                 clamped[x_out(s, 3), inner] = as_float(r.in_x[s, 9:12])
+
+        for sx in range(2):
+            for sy in range(2):
+
+                @pl.when(c_dev(sx, sy)[0])
+                def _(sx=sx, sy=sy):
+                    for _, pad, deep, n, at in corner[-2:]:
+                        plane = HX - deep if sx == 0 else HX + nx - 1 + deep
+                        at = at - 16
+                        pad[plane, y_out(sy, n)] = as_float(r.in_kf[sx * 2 + sy, at : at + n])
 
     def unpack_tough():
         last_one.received()
@@ -519,17 +554,24 @@
             n = nx - 2 * skip
             return lax.fori_loop(HX + skip, HX + nx - skip, body, carry, unroll=part(n, most))
 
-        def outward(far, body, carry):
+        def outward(far, body, carry, n=5):
             def both(i, carry):
                 carry = body(HX - far + i, carry)
-                return body(HX + nx + far - 5 + i, carry)
-
-            return lax.fori_loop(0, 5, both, carry, unroll=True)
-
+                return body(HX + nx + far - n + i, carry)
+
+            return lax.fori_loop(0, n, both, carry, unroll=True)
+
+        own = jnp.zeros((ny, nz), jnp.float32)
         unpack_y()
         inward(1, stiffen, 0, 14)
+        unpack_y_clamp()
         total = inward(2, move, jnp.zeros(shape, jnp.float32), 12)
+        unpack_y_tough()
         inward(3, damage, 0, 5)
+        if sections > 1:
+            stiffen1, mover1 = stages(1)
+            inward(3, stiffen1, 0, 10)
+            own = inward(4, mover1(OY, ny), own, 8)
         unpack_x()
         outward(4, stiffen, 0)
         unpack_clamp()
@@ -537,6 +579,10 @@
         add_up(0, total)
         unpack_tough()
         outward(2, damage, 0)
+        if sections > 1:
+            outward(2, stiffen1, 0)
+            own = outward(0, mover1(OY, ny), own, 4)
+        return own
 
     def send_sums():
         for k, peer in enumerate(peers):
@@ -549,12 +595,9 @@
                 device_id_type=MESH,
             ).start()
 
-    def sweep(rnd):
+    def stages(rnd):
         p = rnd % 2
         q = 1 - p
-        done = rnd == sections - 1
-        tough = r.tough_in.at[rnd - 1]
-
         shape = (wide, nz)
         first, last = lanes(shape, 0), lanes(shape, nz - 1)
         row_inside = inside_rows(shape, 2)
@@ -573,8 +616,6 @@
                 jnp.logical_and(row_inside, inside_plane(xp)), half * div, 0.0
             )
             return carry
-
-        lax.fori_loop(HX - 2, HX + nx + 2, stiffen, 0, unroll=part(nx + 4, 10))
 
         def mover(b, n):
             shape = (n, nz)
@@ -597,9 +638,20 @@
 
             return move
 
-        total = lax.fori_loop(
-            HX, HX + nx, mover(OY, ny), jnp.zeros((ny, nz), jnp.float32), unroll=part(nx, 8)
-        )
+        return stiffen, mover
+
+    def sweep(rnd, total):
+        p = rnd % 2
+        q = 1 - p
+        done = rnd == sections - 1
+        tough = r.tough_in.at[rnd - 1]
+
+        stiffen, mover = stages(rnd)
+        if rnd > 1:
+            lax.fori_loop(HX - 2, HX + nx + 2, stiffen, 0, unroll=part(nx + 4, 10))
+            total = lax.fori_loop(
+                HX, HX + nx, mover(OY, ny), jnp.zeros((ny, nz), jnp.float32), unroll=part(nx, 8)
+            )
         add_up(rnd, total)
         if done:
             send_sums()
@@ -764,11 +816,11 @@
                 def _(sx=sx, sy=sy):
                     state[q, 3, x_out(sx, 1), y_out(sy, 2)] = r.in_d_c[par, sx * 2 + sy]
 
-    open_sweep()
+    total = open_sweep()
     if sections == 1:
         send_sums()
     for rnd in range(1, sections):
-        sweep(rnd)
+        sweep(rnd, total)
 
     cells = 3.0 * nx * ngx * ny * ngy * nz
     beside_y.sent()
@@ -777,14 +829,14 @@
     last_one.sent()
     for copy in tough_copies:
         copy.wait_send()
-    for k in range(1, group):
-        other = lax.rem(me + k, group)
+    for k, peer in enumerate(peers):
+        other = peer["gx"] * ngy + peer["gy"]
         pltpu.make_async_remote_copy(
             src_ref=r.sums.at[me],
             dst_ref=r.sums.at[other],
-            send_sem=r.sum_send.at[k - 1],
+            send_sem=r.sum_send.at[k],
             recv_sem=r.sum_recv.at[other],
-            device_id=peers[k - 1],
+            device_id=peer,
             device_id_type=MESH,
         ).wait()
     total = r.sums[0]
@@ -843,25 +895,29 @@
         "tough_pad": vmem(padded, f32),
         "crack_pad": vmem(padded, f32),
         "tough_in": vmem((later, nx, ny, nz), f32),
-        "pack_l": vmem((2, nx, 8, nz), jnp.int32),
+        "pack_l": vmem((2, 5 * nx, nz), jnp.int32),
+        "pack_f": vmem((2, 3 * nx, nz), jnp.int32),
         "pack_c": vmem((2, nx, 4, nz), jnp.int32),
         "pack_t": vmem((2, nx, 2, nz), f32),
-        "pack_k": vmem((4, 3, 8, nz), jnp.int32),
+        "pack_k": vmem((4, 16, nz), jnp.int32),
+        "pack_kf": vmem((4, 4, nz), jnp.int32),
         "pack_tk": vmem((4, 1, nz), f32),
         "in_x": vmem((2, 12, ny, nz), jnp.int32),
         "in_tx": vmem((2, 2, ny, nz), f32),
-        "in_l": vmem((2, nx, 8, nz), jnp.int32),
+        "in_l": vmem((2, 5 * nx, nz), jnp.int32),
+        "in_f": vmem((2, 3 * nx, nz), jnp.int32),
         "in_c": vmem((2, nx, 4, nz), jnp.int32),
         "in_ty": vmem((2, nx, 2, nz), f32),
-        "in_k": vmem((4, 3, 8, nz), jnp.int32),
+        "in_k": vmem((4, 16, nz), jnp.int32),
+        "in_kf": vmem((4, 4, nz), jnp.int32),
         "in_tk": vmem((4, 1, nz), f32),
         "sums": vmem((group, sections, nz), f32),
-        "y_send": dma((6,)),
-        "y_recv": dma((6,)),
+        "y_send": dma((8,)),
+        "y_recv": dma((8,)),
         "early_send": dma((8,)),
         "early_recv": dma((8,)),
-        "later_send": dma((2,)),
-        "later_recv": dma((2,)),
+        "later_send": dma((6,)),
+        "later_recv": dma((6,)),
         "last_send": dma((6,)),
         "last_recv": dma((6,)),
         "tough_send": dma((later,)),

time: 19.3 us -> 18.8 us (0.974)
  Pallas kernels: 17.8 us -> 17.3 us
    pallas_call x1, Pallas kernels: 16.5 us -> 16 us  [on_device(): pl.pallas_call(functools.partial(kernel, (sections, ngx, ngy, nx, ny, nz)...]
where the time goes in v4:
time: 18.8 us; the launch traced here: 18.6 us
  Pallas kernels  17.3 us (92%)
  between operations  1.28 us (7%)
    pallas_call x1, Pallas kernels, on_device(): pl.pallas_call(functools.partial(kernel, (sections, ngx, ngy, nx, ny, nz)...  16 us
    pallas_call x1, Pallas kernels, on_device(): pl.pallas_call(put_out, out_shape=(jax.ShapeDtypeStruct((1, 3, nx, ny, nz...  1.33 us

profile of v4, /device:TPU:0, one launch (start us, length us, event | category | flops | bytes accessed | tf_op | source)
XLA Modules:
  0.0 18.6 jit_solution(15825778808622973957)
XLA Ops:
  1.3 16.0 %shard_map.85 = (f32[16,16,128]{2,1,0:T(8,128)S(1)}, f32[16,16,128]{2,1,0:T(8,128)S(1)}, f32[16,16,128]{2,1,0:T(8,128)S(1)}, f32[16,16,128]{2,1,0:T(8,128)S(1)}, f32[1,2]{1,0:T(1,128)S(1)}) custom-call(s32[1]{0:T(128)S(6)} %copy.9.refs_0_, f32[3,64]{1,0:T(4,128)} %bitcast.1, f32[1,16,16,128]{3,2,1,0:T(8,128)} %refs_2_.1, s32[16,16,128]{2,1,0:T(8,128)} %refs_3_.1, ...), custom_call_target="tpu_custom_call" | custom-call | tf_op jit(solution)/shard_map/pallas_call | solution.py:949
  17.3 1.3 %shard_map.86 = (f32[1,3,16,16,128]{4,3,2,1,0:T(8,128)}, f32[1,16,16,128]{3,2,1,0:T(8,128)}, f32[1,2]{1,0:T(1,128)}) custom-call(f32[16,16,128]{2,1,0:T(8,128)S(1)} %get-tuple-element.8.first_ref, f32[16,16,128]{2,1,0:T(8,128)S(1)} %get-tuple-element.9.second_ref, f32[16,16,128]{2,1,0:T(8,128)S(1)} %get-tuple-element.10.third_ref, ...), custom_call_target="tpu_custom_call" | custom-call | tf_op jit(solution)/shard_map/pallas_call | solution.py:962

commit v5 on v4

--- a/solution.py
+++ b/solution.py
@@ -83,7 +83,7 @@
     sections, ngx, ngy, nx, ny, nz = sizes
     r = types.SimpleNamespace(**dict(zip(names, refs)))
     local, state, stiff, flow = r.local, r.state, r.stiff, r.flow
-    held, clamped, free, tough_pad, crack_pad = r.held, r.clamped, r.free, r.tough_pad, r.crack_pad
+    held, clamped, tough_pad, crack_pad = r.held, r.clamped, r.tough_pad, r.crack_pad
     load_ref, crack_ref, clamp_ref, tough_ref = r.load_ref, r.crack_ref, r.clamp_ref, r.tough_ref
     disp_refs = (r.first_ref, r.second_ref, r.third_ref)
     sec = lax.axis_index("section")
@@ -186,8 +186,8 @@
             for cond, _, back in self.items[begin:end]:
                 pl.when(cond)(back.wait_recv)
 
-        def sent(self):
-            for cond, copy, _ in self.items:
+        def sent(self, begin=0, end=None):
+            for cond, copy, _ in self.items[begin:end]:
                 pl.when(cond)(copy.wait_send)
 
     rows = ny + 2 * OY
@@ -198,7 +198,6 @@
         crack_pad[xp] = zero
         clamped[xp] = zero + 1.0
         tough_pad[xp] = zero + 1.0
-        free[xp] = zero
         if sections > 2:
             for p in range(2):
                 for f in range(4):
@@ -293,9 +292,6 @@
             r.pack_tk[sx * 2 + sy] = tough_ref[0, 0 if sx == 0 else nx - 1, row : row + 1]
     beside_y.start(6)
     early.start(4)
-    later.start()
-    last_one.start()
-
     tough_copies = []
     for k in range(1, sections):
         copy = pltpu.make_async_remote_copy(
@@ -313,11 +309,8 @@
     as_float = lambda v: v.astype(jnp.float32)
 
     def fill(x, carry):
-        load = as_float(load_ref[x])
-        clamp = as_float(clamp_ref[x])
-        held[x + HX, inner] = load
-        clamped[x + HX, inner] = clamp
-        free[x + HX, inner] = 1.0 - jnp.maximum(clamp, load)
+        held[x + HX, inner] = as_float(load_ref[x])
+        clamped[x + HX, inner] = as_float(clamp_ref[x])
         crack_pad[x + HX, inner] = as_float(crack_ref[x])
         tough_pad[x + HX, inner] = tough_ref[0, x]
         return carry
@@ -499,42 +492,51 @@
     def add_up(rnd, total):
         r.sums[me, rnd : rnd + 1] = jnp.sum(total, axis=0, keepdims=True)
 
-    def open_sweep():
-        shape = (deep, nz)
+    def open_stages(above, n):
+        shape = (n, nz)
         first, last = lanes(shape, 0), lanes(shape, nz - 1)
-        row_inside = inside_rows(shape, 4)
-        a = OY - 4
+        row_inside = inside_rows(shape, above)
+        row = lax.broadcasted_iota(jnp.int32, shape, 0)
+        a = OY - above
 
         def stiffen(xp, carry):
-            half = 0.5 * (jnp.square(1.0 - crack_pad[xp, a : a + deep]) + stiff_floor)
-            stiff[xp, a : a + deep] = half
-            up, down = beside(held[xp, a : a + deep], 0.0, first, last)
+            half = 0.5 * (jnp.square(1.0 - crack_pad[xp, a : a + n]) + stiff_floor)
+            stiff[xp, a : a + n] = half
+            up, down = beside(held[xp, a : a + n], 0.0, first, last)
             div = (
-                vector[0] * (held[xp + 1, a : a + deep] - held[xp - 1, a : a + deep])
-                + vector[1] * (held[xp, a + 1 : a + 1 + deep] - held[xp, a - 1 : a - 1 + deep])
+                vector[0] * (held[xp + 1, a : a + n] - held[xp - 1, a : a + n])
+                + vector[1] * (held[xp, a + 1 : a + 1 + n] - held[xp, a - 1 : a - 1 + n])
                 + vector[2] * (up - down)
             )
-            flow[xp, a : a + deep] = jnp.where(
+            flow[xp, a : a + n] = jnp.where(
                 jnp.logical_and(row_inside, inside_plane(xp)), half * div, 0.0
             )
             return carry
 
-        def move(xp, total):
-            at = lambda ref, dx, dy: ref[xp + dx, a + dy : a + dy + deep]
-            pairs, weights, faces, grads = elastic(at, first, last)
-            load, spread = laplace(at, held, faces, weights, first, last)
-            pin = at(clamped, 0, 0) + load > 0.5
-            squares = None
-            for f in range(3):
-                res = vector[f] * spread + grads[f]
-                moved = jnp.where(pin, 0.0, relax_weight * res / (weights + pairs[f]))
-                state[1, f, xp, a : a + deep] = vector[f] * load + moved
-                square = res * res
-                squares = square if squares is None else squares + square
-            return total + jnp.where(at(free, 0, 0) > 0.5, squares, 0.0)
+        def mover(low, high):
+            def move(xp, total):
+                at = lambda ref, dx, dy: ref[xp + dx, a + dy : a + dy + n]
+                pairs, weights, faces, grads = elastic(at, first, last)
+                load, spread = laplace(at, held, faces, weights, first, last)
+                pin = at(clamped, 0, 0) + load > 0.5
+                squares = None
+                for f in range(3):
+                    res = vector[f] * spread + grads[f]
+                    moved = jnp.where(pin, 0.0, relax_weight * res / (weights + pairs[f]))
+                    state[1, f, xp, a : a + n] = vector[f] * load + moved
+                    square = res * res
+                    squares = square if squares is None else squares + square
+                if low >= high:
+                    return total
+                counted = jnp.logical_and(row >= low + above, row < high + above)
+                return total + jnp.where(
+                    jnp.logical_and(counted, jnp.logical_not(pin)), squares, 0.0
+                )
+
+            return move
 
         def damage(xp, carry):
-            at = lambda ref, dx, dy: ref[xp + dx, a + dy : a + dy + deep]
+            at = lambda ref, dx, dy: ref[xp + dx, a + dy : a + dy + n]
             energy = strain_energy(at, state.at[1], lambda f, v: None, first, last)
             renewed = renew(
                 at,
@@ -545,43 +547,72 @@
                 first,
                 last,
             )
-            state[1, 3, xp, a : a + deep] = jnp.where(
+            state[1, 3, xp, a : a + n] = jnp.where(
                 jnp.logical_and(row_inside, inside_plane(xp)), renewed, 0.0
             )
             return carry
 
+        return stiffen, mover, damage
+
+    def open_sweep():
         def inward(skip, body, carry, most):
             n = nx - 2 * skip
             return lax.fori_loop(HX + skip, HX + nx - skip, body, carry, unroll=part(n, most))
 
-        def outward(far, body, carry, n=5):
+        def outward(far, n, body, carry):
             def both(i, carry):
                 carry = body(HX - far + i, carry)
                 return body(HX + nx + far - n + i, carry)
 
             return lax.fori_loop(0, n, both, carry, unroll=True)
 
-        own = jnp.zeros((ny, nz), jnp.float32)
+        def pair(one, two):
+            def body(xp, carry):
+                return one(xp, carry[0]), two(xp, carry[1])
+
+            return body
+
+        blank = lambda n: jnp.zeros((n, nz), jnp.float32)
+        fold = lambda v: jnp.sum(v, axis=0, keepdims=True)
+
+        stiffen, mover, damage = open_stages(0, ny)
+        inward(1, stiffen, 0, 14)
+        inside = inward(2, mover(2, ny - 2), blank(ny), 12)
+        inward(3, damage, 0, 5)
+
+        early.sent(0, 4)
+        later.start()
+        last_one.start()
+
+        low = open_stages(4, 8)
+        high = open_stages(4 - ny, 8)
         unpack_y()
-        inward(1, stiffen, 0, 14)
+        inward(1, pair(low[0], high[0]), (0, 0), 14)
         unpack_y_clamp()
-        total = inward(2, move, jnp.zeros(shape, jnp.float32), 12)
+        rims = inward(
+            2, pair(low[1](0, 2), high[1](ny - 2, ny)), (blank(8), blank(8)), 12
+        )
         unpack_y_tough()
-        inward(3, damage, 0, 5)
+        inward(3, pair(low[2], high[2]), (0, 0), 5)
+        own = blank(ny)
         if sections > 1:
             stiffen1, mover1 = stages(1)
             inward(3, stiffen1, 0, 10)
             own = inward(4, mover1(OY, ny), own, 8)
+
         unpack_x()
-        outward(4, stiffen, 0)
+        stiffen, mover, damage = open_stages(4, deep)
+        outward(4, 5, stiffen, 0)
+        ends = outward(0, 2, mover(0, ny), blank(deep))
         unpack_clamp()
-        total = outward(3, move, total)
-        add_up(0, total)
+        outward(3, 3, mover(0, 0), blank(deep))
+        r.sums[me, 0:1] = fold(inside) + fold(rims[0] + rims[1]) + fold(ends)
+        outward(0, 3, damage, 0)
         unpack_tough()
-        outward(2, damage, 0)
+        outward(2, 2, damage, 0)
         if sections > 1:
-            outward(2, stiffen1, 0)
-            own = outward(0, mover1(OY, ny), own, 4)
+            outward(2, 5, stiffen1, 0)
+            own = outward(0, 4, mover1(OY, ny), own)
         return own
 
     def send_sums():
@@ -824,7 +855,7 @@
 
     cells = 3.0 * nx * ngx * ny * ngy * nz
     beside_y.sent()
-    early.sent()
+    early.sent(4)
     later.sent()
     last_one.sent()
     for copy in tough_copies:
@@ -891,7 +922,6 @@
         "flow": vmem(padded, f32),
         "held": vmem(padded, f32),
         "clamped": vmem(padded, f32),
-        "free": vmem(padded, f32),
         "tough_pad": vmem(padded, f32),
         "crack_pad": vmem(padded, f32),
         "tough_in": vmem((later, nx, ny, nz), f32),

time: 18.8 us -> 19.2 us (1.021)
  Pallas kernels: 17.3 us -> 17.7 us
    pallas_call x1, Pallas kernels: 16 us -> 16.4 us  [on_device(): pl.pallas_call(functools.partial(kernel, (sections, ngx, ngy, nx, ny, nz)...]
where the time goes in v5:
time: 19.2 us; the launch traced here: 19 us
  Pallas kernels  17.7 us (92%)
  between operations  1.28 us (7%)
    pallas_call x1, Pallas kernels, on_device(): pl.pallas_call(functools.partial(kernel, (sections, ngx, ngy, nx, ny, nz)...  16.4 us
    pallas_call x1, Pallas kernels, on_device(): pl.pallas_call(put_out, out_shape=(jax.ShapeDtypeStruct((1, 3, nx, ny, nz...  1.33 us

profile of v5, /device:TPU:0, one launch (start us, length us, event | category | flops | bytes accessed | tf_op | source)
XLA Modules:
  0.0 19.0 jit_solution(15628970436911512457)
XLA Ops:
  1.3 16.4 %shard_map.85 = (f32[16,16,128]{2,1,0:T(8,128)S(1)}, f32[16,16,128]{2,1,0:T(8,128)S(1)}, f32[16,16,128]{2,1,0:T(8,128)S(1)}, f32[16,16,128]{2,1,0:T(8,128)S(1)}, f32[1,2]{1,0:T(1,128)S(1)}) custom-call(s32[1]{0:T(128)S(6)} %copy.9.refs_0_, f32[3,64]{1,0:T(4,128)} %bitcast.1, f32[1,16,16,128]{3,2,1,0:T(8,128)} %refs_2_.1, s32[16,16,128]{2,1,0:T(8,128)} %refs_3_.1, ...), custom_call_target="tpu_custom_call" | custom-call | tf_op jit(solution)/shard_map/pallas_call | solution.py:979
  17.7 1.3 %shard_map.86 = (f32[1,3,16,16,128]{4,3,2,1,0:T(8,128)}, f32[1,16,16,128]{3,2,1,0:T(8,128)}, f32[1,2]{1,0:T(1,128)}) custom-call(f32[16,16,128]{2,1,0:T(8,128)S(1)} %get-tuple-element.8.first_ref, f32[16,16,128]{2,1,0:T(8,128)S(1)} %get-tuple-element.9.second_ref, f32[16,16,128]{2,1,0:T(8,128)S(1)} %get-tuple-element.10.third_ref, ...), custom_call_target="tpu_custom_call" | custom-call | tf_op jit(solution)/shard_map/pallas_call | solution.py:992

commit v6 on v5

--- a/solution.py
+++ b/solution.py
@@ -215,41 +215,57 @@
         for x in range(nx):
             r.pack_l[s, 5 * x : 5 * x + 5] = load_ref[x, side(5)]
             r.pack_f[s, 3 * x : 3 * x + 3] = clamp_ref[x, side(3)]
-    corner = (
+    near_corner = (
         (load_ref, held, 1, 4, 0),
         (load_ref, held, 2, 3, 4),
-        (load_ref, held, 4, 1, 7),
-        (load_ref, held, 3, 2, 8),
-        (crack_ref, crack_pad, 1, 3, 10),
-        (crack_ref, crack_pad, 2, 2, 13),
-        (crack_ref, crack_pad, 3, 1, 15),
-        (clamp_ref, clamped, 1, 2, 16),
-        (clamp_ref, clamped, 2, 1, 18),
+        (load_ref, held, 3, 2, 7),
+        (crack_ref, crack_pad, 1, 3, 9),
+        (crack_ref, crack_pad, 2, 2, 12),
+        (clamp_ref, clamped, 1, 2, 14),
     )
+    far_corner = (
+        (load_ref, held, 4, 1, 0),
+        (crack_ref, crack_pad, 3, 1, 1),
+        (clamp_ref, clamped, 2, 1, 2),
+    )
+
+    def x_from(s, deep):
+        return deep - 1 if s == 0 else nx - deep
+
+    def x_at(s, deep):
+        return HX - deep if s == 0 else HX + nx - 1 + deep
+
     for sx in range(2):
         for sy in range(2):
-            for ref, _, deep, n, at in corner:
-                plane = deep - 1 if sx == 0 else nx - deep
-                first = 0 if sy == 0 else ny - n
-                pack, at = (r.pack_k, at) if at < 16 else (r.pack_kf, at - 16)
-                pack[sx * 2 + sy, at : at + n] = ref[plane, first : first + n]
+            for pack, corner in ((r.pack_k, near_corner), (r.pack_kf, far_corner)):
+                for ref, _, deep, n, at in corner:
+                    first = 0 if sy == 0 else ny - n
+                    pack[sx * 2 + sy, at : at + n] = ref[x_from(sx, deep), first : first + n]
 
     pl.semaphore_wait(barrier, group - 1 + sections - 1)
 
     beside_y = Exchange(r.y_send, r.y_recv)
-    early = Exchange(r.early_send, r.early_recv)
-    later = Exchange(r.later_send, r.later_recv)
-    last_one = Exchange(r.last_send, r.last_recv)
-    for s in range(2):
-        for ex, ref, buf, width, at, slot in (
-            (early, load_ref, r.in_x, 5, 0, 0),
-            (early, crack_ref, r.in_x, 4, 5, 2),
-            (later, clamp_ref, r.in_x, 3, 9, 0),
-            (last_one, tough_ref.at[0], r.in_tx, 2, 0, 0),
-        ):
+    part_a = Exchange(r.a_send, r.a_recv)
+    part_b = Exchange(r.b_send, r.b_recv)
+    part_c = Exchange(r.c_send, r.c_recv)
+    for ex, ref, buf, deep, width, at, slot in (
+        (part_a, load_ref, r.in_a, 3, 3, 0, 0),
+        (part_a, crack_ref, r.in_a, 2, 2, 3, 2),
+        (part_a, clamp_ref, r.in_a, 1, 1, 5, 4),
+        (part_b, load_ref, r.in_b, 4, 1, 0, 0),
+        (part_b, crack_ref, r.in_b, 3, 1, 1, 2),
+        (part_b, clamp_ref, r.in_b, 2, 1, 2, 4),
+        (part_b, tough_ref.at[0], r.in_tx, 1, 1, 0, 6),
+        (part_c, load_ref, r.in_c_x, 5, 1, 0, 0),
+        (part_c, crack_ref, r.in_c_x, 4, 1, 1, 2),
+        (part_c, clamp_ref, r.in_c_x, 3, 1, 2, 4),
+        (part_c, tough_ref.at[0], r.in_tx, 2, 1, 1, 6),
+    ):
+        for s in range(2):
+            first = deep - width if s == 0 else nx - deep
             ex.add(
                 x_dev(s),
-                ref.at[pl.ds(0 if s == 0 else nx - width, width)],
+                ref.at[pl.ds(first, width)],
                 buf.at[1 - s, pl.ds(at, width)],
                 buf.at[s, pl.ds(at, width)],
                 slot + 1 - s,
@@ -269,19 +285,16 @@
     for sx in range(2):
         for sy in range(2):
             here, away = sx * 2 + sy, (1 - sx) * 2 + 1 - sy
-            early.add(
-                c_dev(sx, sy), r.pack_k.at[here], r.in_k.at[away], r.in_k.at[here],
-                4 + away, 4 + here,
-            )
-            later.add(
-                c_dev(sx, sy), r.pack_kf.at[here], r.in_kf.at[away], r.in_kf.at[here],
-                2 + away, 2 + here,
-            )
-            last_one.add(
-                c_dev(sx, sy), r.pack_tk.at[here], r.in_tk.at[away], r.in_tk.at[here],
-                2 + away, 2 + here,
-            )
-    early.start(0, 4)
+            for ex, pack, buf, slot in (
+                (part_a, r.pack_k, r.in_k, 6),
+                (part_b, r.pack_kf, r.in_kf, 8),
+                (part_b, r.pack_tk, r.in_tk, 12),
+            ):
+                ex.add(
+                    c_dev(sx, sy), pack.at[here], buf.at[away], buf.at[here],
+                    slot + away, slot + here,
+                )
+    part_a.start(0, 6)
     beside_y.start(0, 6)
     fetch[3].wait()
     for s in range(2):
@@ -291,7 +304,9 @@
             row = 0 if sy == 0 else ny - 1
             r.pack_tk[sx * 2 + sy] = tough_ref[0, 0 if sx == 0 else nx - 1, row : row + 1]
     beside_y.start(6)
-    early.start(4)
+    part_a.start(6)
+    part_b.start()
+    part_c.start()
     tough_copies = []
     for k in range(1, sections):
         copy = pltpu.make_async_remote_copy(
@@ -357,57 +372,52 @@
             def _(s=s):
                 tough_pad[planes, y_out(s, 2)] = r.in_ty[s]
 
-    def unpack_x():
-        early.received()
+    def unpack_corners(corner, buf):
+        for sx in range(2):
+            for sy in range(2):
+
+                @pl.when(c_dev(sx, sy)[0])
+                def _(sx=sx, sy=sy):
+                    for _, pad, deep, n, at in corner:
+                        pad[x_at(sx, deep), y_out(sy, n)] = as_float(
+                            buf[sx * 2 + sy, at : at + n]
+                        )
+
+    def unpack_a():
+        part_a.received()
         for s in range(2):
 
             @pl.when(there["gx"][s])
             def _(s=s):
-                held[x_out(s, 5), inner] = as_float(r.in_x[s, 0:5])
-                crack_pad[x_out(s, 4), inner] = as_float(r.in_x[s, 5:9])
-
+                held[x_out(s, 3), inner] = as_float(r.in_a[s, 0:3])
+                crack_pad[x_out(s, 2), inner] = as_float(r.in_a[s, 3:5])
+                clamped[x_out(s, 1), inner] = as_float(r.in_a[s, 5:6])
+
+        unpack_corners(near_corner, r.in_k)
+
+    def unpack_far(part, buf, less):
+        part.received()
+        for s in range(2):
+
+            @pl.when(there["gx"][s])
+            def _(s=s):
+                held[x_at(s, 5 - less), inner] = as_float(buf[s, 0])
+                crack_pad[x_at(s, 4 - less), inner] = as_float(buf[s, 1])
+                clamped[x_at(s, 3 - less), inner] = as_float(buf[s, 2])
+                tough_pad[x_at(s, 2 - less), inner] = r.in_tx[s, 1 - less]
+
+    def unpack_b():
+        unpack_far(part_b, r.in_b, 1)
+        unpack_corners(far_corner, r.in_kf)
         for sx in range(2):
             for sy in range(2):
 
                 @pl.when(c_dev(sx, sy)[0])
                 def _(sx=sx, sy=sy):
-                    for _, pad, deep, n, at in corner[:-2]:
-                        plane = HX - deep if sx == 0 else HX + nx - 1 + deep
-                        pad[plane, y_out(sy, n)] = as_float(r.in_k[sx * 2 + sy, at : at + n])
-
-    def unpack_clamp():
-        later.received()
-        for s in range(2):
-
-            @pl.when(there["gx"][s])
-            def _(s=s):
-                clamped[x_out(s, 3), inner] = as_float(r.in_x[s, 9:12])
-
-        for sx in range(2):
-            for sy in range(2):
-
-                @pl.when(c_dev(sx, sy)[0])
-                def _(sx=sx, sy=sy):
-                    for _, pad, deep, n, at in corner[-2:]:
-                        plane = HX - deep if sx == 0 else HX + nx - 1 + deep
-                        at = at - 16
-                        pad[plane, y_out(sy, n)] = as_float(r.in_kf[sx * 2 + sy, at : at + n])
-
-    def unpack_tough():
-        last_one.received()
-        for s in range(2):
-
-            @pl.when(there["gx"][s])
-            def _(s=s):
-                tough_pad[x_out(s, 2), inner] = r.in_tx[s]
-
-        for sx in range(2):
-            for sy in range(2):
-
-                @pl.when(c_dev(sx, sy)[0])
-                def _(sx=sx, sy=sy):
-                    plane = HX - 1 if sx == 0 else HX + nx
-                    tough_pad[plane, y_out(sy, 1)] = r.in_tk[sx * 2 + sy]
+                    tough_pad[x_at(sx, 1), y_out(sy, 1)] = r.in_tk[sx * 2 + sy]
+
+    def unpack_c():
+        unpack_far(part_c, r.in_c_x, 0)
 
     wide = up8(ny + 4)
     deep = up8(ny + 8)
@@ -580,10 +590,6 @@
         inside = inward(2, mover(2, ny - 2), blank(ny), 12)
         inward(3, damage, 0, 5)
 
-        early.sent(0, 4)
-        later.start()
-        last_one.start()
-
         low = open_stages(4, 8)
         high = open_stages(4 - ny, 8)
         unpack_y()
@@ -594,26 +600,36 @@
         )
         unpack_y_tough()
         inward(3, pair(low[2], high[2]), (0, 0), 5)
-        own = blank(ny)
-        if sections > 1:
-            stiffen1, mover1 = stages(1)
-            inward(3, stiffen1, 0, 10)
-            own = inward(4, mover1(OY, ny), own, 8)
-
-        unpack_x()
+        stiffen1, mover1 = stages(1)
+        move1 = mover1(OY, ny)
+        inward(3, stiffen1, 0, 10)
+        own = inward(4, move1, blank(ny), 8)
+
         stiffen, mover, damage = open_stages(4, deep)
-        outward(4, 5, stiffen, 0)
+        unpack_a()
+        outward(2, 3, stiffen, 0)
         ends = outward(0, 2, mover(0, ny), blank(deep))
-        unpack_clamp()
-        outward(3, 3, mover(0, 0), blank(deep))
+        outward(1, 1, mover(0, 0), blank(deep))
         r.sums[me, 0:1] = fold(inside) + fold(rims[0] + rims[1]) + fold(ends)
         outward(0, 3, damage, 0)
-        unpack_tough()
-        outward(2, 2, damage, 0)
-        if sections > 1:
-            outward(2, 5, stiffen1, 0)
-            own = outward(0, 4, mover1(OY, ny), own)
-        return own
+        outward(0, 3, stiffen1, 0)
+        own = outward(-1, 3, move1, own)
+
+        unpack_b()
+        outward(3, 1, stiffen, 0)
+        outward(2, 1, mover(0, 0), blank(deep))
+        outward(1, 1, damage, 0)
+        outward(1, 1, stiffen1, 0)
+        own = outward(0, 1, move1, own)
+
+        def finish():
+            unpack_c()
+            outward(4, 1, stiffen, 0)
+            outward(3, 1, mover(0, 0), blank(deep))
+            outward(2, 1, damage, 0)
+            outward(2, 1, stiffen1, 0)
+
+        return own, finish
 
     def send_sums():
         for k, peer in enumerate(peers):
@@ -686,6 +702,8 @@
         add_up(rnd, total)
         if done:
             send_sums()
+        if rnd == 1:
+            finish_open()
         none = jnp.zeros((8, nz), jnp.float32)
 
         def edges(xp, carry):
@@ -847,17 +865,15 @@
                 def _(sx=sx, sy=sy):
                     state[q, 3, x_out(sx, 1), y_out(sy, 2)] = r.in_d_c[par, sx * 2 + sy]
 
-    total = open_sweep()
-    if sections == 1:
-        send_sums()
+    total, finish_open = open_sweep()
     for rnd in range(1, sections):
         sweep(rnd, total)
 
     cells = 3.0 * nx * ngx * ny * ngy * nz
     beside_y.sent()
-    early.sent(4)
-    later.sent()
-    last_one.sent()
+    part_a.sent()
+    part_b.sent()
+    part_c.sent()
     for copy in tough_copies:
         copy.wait_send()
     for k, peer in enumerate(peers):
@@ -932,7 +948,9 @@
         "pack_k": vmem((4, 16, nz), jnp.int32),
         "pack_kf": vmem((4, 4, nz), jnp.int32),
         "pack_tk": vmem((4, 1, nz), f32),
-        "in_x": vmem((2, 12, ny, nz), jnp.int32),
+        "in_a": vmem((2, 6, ny, nz), jnp.int32),
+        "in_b": vmem((2, 3, ny, nz), jnp.int32),
+        "in_c_x": vmem((2, 3, ny, nz), jnp.int32),
         "in_tx": vmem((2, 2, ny, nz), f32),
         "in_l": vmem((2, 5 * nx, nz), jnp.int32),
         "in_f": vmem((2, 3 * nx, nz), jnp.int32),
@@ -944,12 +962,12 @@
         "sums": vmem((group, sections, nz), f32),
         "y_send": dma((8,)),
         "y_recv": dma((8,)),
-        "early_send": dma((8,)),
-        "early_recv": dma((8,)),
-        "later_send": dma((6,)),
-        "later_recv": dma((6,)),
-        "last_send": dma((6,)),
-        "last_recv": dma((6,)),
+        "a_send": dma((10,)),
+        "a_recv": dma((10,)),
+        "b_send": dma((16,)),
+        "b_recv": dma((16,)),
+        "c_send": dma((8,)),
+        "c_recv": dma((8,)),
         "tough_send": dma((later,)),
         "tough_recv": dma((later,)),
         "sum_send": dma((max(group - 1, 1),)),

time: 19.2 us -> 18.5 us (0.964)
  Pallas kernels: 17.7 us -> 17 us
    pallas_call x1, Pallas kernels: 16.4 us -> 15.7 us  [on_device(): pl.pallas_call(functools.partial(kernel, (sections, ngx, ngy, nx, ny, nz)...]
where the time goes in v6:
time: 18.5 us; the launch traced here: 18.3 us
  Pallas kernels  17 us (92%)
  between operations  1.28 us (7%)
    pallas_call x1, Pallas kernels, on_device(): pl.pallas_call(functools.partial(kernel, (sections, ngx, ngy, nx, ny, nz)...  15.7 us
    pallas_call x1, Pallas kernels, on_device(): pl.pallas_call(put_out, out_shape=(jax.ShapeDtypeStruct((1, 3, nx, ny, nz...  1.33 us

profile of v6, /device:TPU:0, one launch (start us, length us, event | category | flops | bytes accessed | tf_op | source)
XLA Modules:
  0.0 18.3 jit_solution(16454939281457343916)
XLA Ops:
  1.3 15.7 %shard_map.85 = (f32[16,16,128]{2,1,0:T(8,128)S(1)}, f32[16,16,128]{2,1,0:T(8,128)S(1)}, f32[16,16,128]{2,1,0:T(8,128)S(1)}, f32[16,16,128]{2,1,0:T(8,128)S(1)}, f32[1,2]{1,0:T(1,128)S(1)}) custom-call(s32[1]{0:T(128)S(6)} %copy.9.refs_0_, f32[3,64]{1,0:T(4,128)} %bitcast.1, f32[1,16,16,128]{3,2,1,0:T(8,128)} %refs_2_.1, s32[16,16,128]{2,1,0:T(8,128)} %refs_3_.1, ...), custom_call_target="tpu_custom_call" | custom-call | tf_op jit(solution)/shard_map/pallas_call | solution.py:997
  17.0 1.3 %shard_map.86 = (f32[1,3,16,16,128]{4,3,2,1,0:T(8,128)}, f32[1,16,16,128]{3,2,1,0:T(8,128)}, f32[1,2]{1,0:T(1,128)}) custom-call(f32[16,16,128]{2,1,0:T(8,128)S(1)} %get-tuple-element.8.first_ref, f32[16,16,128]{2,1,0:T(8,128)S(1)} %get-tuple-element.9.second_ref, f32[16,16,128]{2,1,0:T(8,128)S(1)} %get-tuple-element.10.third_ref, ...), custom_call_target="tpu_custom_call" | custom-call | tf_op jit(solution)/shard_map/pallas_call | solution.py:1010

commit v7 on v6

--- a/solution.py
+++ b/solution.py
@@ -98,9 +98,38 @@
     for i, j in offsets:
         peers.append({"gx": lax.rem(gx + i, ngx), "gy": lax.rem(gy + j, ngy)})
 
+    there = {
+        "gx": (gx > 0, gx < ngx - 1),
+        "gy": (gy > 0, gy < ngy - 1),
+    }
+    step = (-1, 1)
+
+    def x_dev(s):
+        return there["gx"][s], {"gx": gx + step[s]}
+
+    def y_dev(s):
+        return there["gy"][s], {"gy": gy + step[s]}
+
+    def c_dev(sx, sy):
+        return (
+            jnp.logical_and(there["gx"][sx], there["gy"][sy]),
+            {"gx": gx + step[sx], "gy": gy + step[sy]},
+        )
+
+    neighbours = [x_dev(s) for s in range(2)] + [y_dev(s) for s in range(2)]
+    neighbours += [c_dev(sx, sy) for sx in range(2) for sy in range(2)]
+    in_line = lambda name: sum(t.astype(jnp.int32) for t in there[name])
+    near_count = (in_line("gx") + 1) * (in_line("gy") + 1) - 1
+
+    def greet(sem):
+        for cond, dev in neighbours:
+
+            @pl.when(cond)
+            def _(dev=dev):
+                pl.semaphore_signal(sem, inc=1, device_id=dev, device_id_type=MESH)
+
     barrier = pltpu.get_barrier_semaphore()
-    for peer in peers:
-        pl.semaphore_signal(barrier, inc=1, device_id=peer, device_id_type=MESH)
+    greet(barrier)
     for k in range(1, sections):
         pl.semaphore_signal(
             barrier,
@@ -124,24 +153,6 @@
     ]
     for copy in fetch:
         copy.start()
-
-    there = {
-        "gx": (gx > 0, gx < ngx - 1),
-        "gy": (gy > 0, gy < ngy - 1),
-    }
-    step = (-1, 1)
-
-    def x_dev(s):
-        return there["gx"][s], {"gx": gx + step[s]}
-
-    def y_dev(s):
-        return there["gy"][s], {"gy": gy + step[s]}
-
-    def c_dev(sx, sy):
-        return (
-            jnp.logical_and(there["gx"][sx], there["gy"][sy]),
-            {"gx": gx + step[sx], "gy": gy + step[sy]},
-        )
 
     class Exchange:
         def __init__(self, send, recv):
@@ -242,7 +253,7 @@
                     first = 0 if sy == 0 else ny - n
                     pack[sx * 2 + sy, at : at + n] = ref[x_from(sx, deep), first : first + n]
 
-    pl.semaphore_wait(barrier, group - 1 + sections - 1)
+    pl.semaphore_wait(barrier, near_count + sections - 1)
 
     beside_y = Exchange(r.y_send, r.y_recv)
     part_a = Exchange(r.a_send, r.a_recv)
@@ -294,8 +305,9 @@
                     c_dev(sx, sy), pack.at[here], buf.at[away], buf.at[here],
                     slot + away, slot + here,
                 )
+    beside_y.start(0, 4)
     part_a.start(0, 6)
-    beside_y.start(0, 6)
+    beside_y.start(4, 6)
     fetch[3].wait()
     for s in range(2):
         r.pack_t[s] = tough_ref[0, :, 0:2] if s == 0 else tough_ref[0, :, ny - 2 : ny]
@@ -383,8 +395,12 @@
                             buf[sx * 2 + sy, at : at + n]
                         )
 
+    further = max(ngx, ngy) - 3
+
     def unpack_a():
         part_a.received()
+        if further > 0:
+            greet(r.reach.at[0])
         for s in range(2):
 
             @pl.when(there["gx"][s])
@@ -632,6 +648,10 @@
         return own, finish
 
     def send_sums():
+        for k in range(further):
+            pl.semaphore_wait(r.reach.at[k], near_count)
+            if k + 1 < further:
+                greet(r.reach.at[k + 1])
         for k, peer in enumerate(peers):
             pltpu.make_async_remote_copy(
                 src_ref=r.sums.at[me],
@@ -968,6 +988,7 @@
         "b_recv": dma((16,)),
         "c_send": dma((8,)),
         "c_recv": dma((8,)),
+        "reach": pltpu.SemaphoreType.REGULAR((max(max(ngx, ngy) - 3, 1),)),
         "tough_send": dma((later,)),
         "tough_recv": dma((later,)),
         "sum_send": dma((max(group - 1, 1),)),

time: 18.5 us -> 19 us (1.027)
  Pallas kernels: 17 us -> 17.6 us
    pallas_call x1, Pallas kernels: 15.7 us -> 16.3 us  [on_device(): pl.pallas_call(functools.partial(kernel, (sections, ngx, ngy, nx, ny, nz)...]
where the time goes in v7:
time: 19 us; the launch traced here: 18.9 us
  Pallas kernels  17.6 us (93%)
  between operations  1.28 us (7%)
    pallas_call x1, Pallas kernels, on_device(): pl.pallas_call(functools.partial(kernel, (sections, ngx, ngy, nx, ny, nz)...  16.3 us
    pallas_call x1, Pallas kernels, on_device(): pl.pallas_call(put_out, out_shape=(jax.ShapeDtypeStruct((1, 3, nx, ny, nz...  1.33 us

profile of v7, /device:TPU:0, one launch (start us, length us, event | category | flops | bytes accessed | tf_op | source)
XLA Modules:
  0.0 18.9 jit_solution(8558648031326190880)
XLA Ops:
  1.3 16.3 %shard_map.85 = (f32[16,16,128]{2,1,0:T(8,128)S(1)}, f32[16,16,128]{2,1,0:T(8,128)S(1)}, f32[16,16,128]{2,1,0:T(8,128)S(1)}, f32[16,16,128]{2,1,0:T(8,128)S(1)}, f32[1,2]{1,0:T(1,128)S(1)}) custom-call(s32[1]{0:T(128)S(6)} %copy.9.refs_0_, f32[3,64]{1,0:T(4,128)} %bitcast.1, f32[1,16,16,128]{3,2,1,0:T(8,128)} %refs_2_.1, s32[16,16,128]{2,1,0:T(8,128)} %refs_3_.1, ...), custom_call_target="tpu_custom_call" | custom-call | tf_op jit(solution)/shard_map/pallas_call | solution.py:1018
  17.5 1.3 %shard_map.86 = (f32[1,3,16,16,128]{4,3,2,1,0:T(8,128)}, f32[1,16,16,128]{3,2,1,0:T(8,128)}, f32[1,2]{1,0:T(1,128)}) custom-call(f32[16,16,128]{2,1,0:T(8,128)S(1)} %get-tuple-element.8.first_ref, f32[16,16,128]{2,1,0:T(8,128)S(1)} %get-tuple-element.9.second_ref, f32[16,16,128]{2,1,0:T(8,128)S(1)} %get-tuple-element.10.third_ref, ...), custom_call_target="tpu_custom_call" | custom-call | tf_op jit(solution)/shard_map/pallas_call | solution.py:1031

commit v8 on v7

--- a/solution.py
+++ b/solution.py
@@ -319,6 +319,9 @@
     part_a.start(6)
     part_b.start()
     part_c.start()
+    further = max(ngx, ngy) - 2
+    if further > 0:
+        greet(r.reach.at[0])
     tough_copies = []
     for k in range(1, sections):
         copy = pltpu.make_async_remote_copy(
@@ -357,32 +360,9 @@
     def y_out(s, n):
         return slice(OY - n, OY) if s == 0 else slice(OY + ny, OY + ny + n)
 
-    def unpack_y():
-        beside_y.received(0, 4)
-        for s in range(2):
-
-            @pl.when(there["gy"][s])
-            def _(s=s):
-                crack_pad[planes, y_out(s, 4)] = as_float(r.in_c[s])
-                for x in range(nx):
-                    held[HX + x, y_out(s, 5)] = as_float(r.in_l[s, 5 * x : 5 * x + 5])
-
-    def unpack_y_clamp():
-        beside_y.received(4, 6)
-        for s in range(2):
-
-            @pl.when(there["gy"][s])
-            def _(s=s):
-                for x in range(nx):
-                    clamped[HX + x, y_out(s, 3)] = as_float(r.in_f[s, 3 * x : 3 * x + 3])
-
-    def unpack_y_tough():
-        beside_y.received(6)
-        for s in range(2):
-
-            @pl.when(there["gy"][s])
-            def _(s=s):
-                tough_pad[planes, y_out(s, 2)] = r.in_ty[s]
+    def from_y(kind, s, put):
+        beside_y.received(2 * kind + s, 2 * kind + s + 1)
+        pl.when(there["gy"][s])(put)
 
     def unpack_corners(corner, buf):
         for sx in range(2):
@@ -395,12 +375,8 @@
                             buf[sx * 2 + sy, at : at + n]
                         )
 
-    further = max(ngx, ngy) - 3
-
     def unpack_a():
         part_a.received()
-        if further > 0:
-            greet(r.reach.at[0])
         for s in range(2):
 
             @pl.when(there["gx"][s])
@@ -592,12 +568,6 @@
 
             return lax.fori_loop(0, n, both, carry, unroll=True)
 
-        def pair(one, two):
-            def body(xp, carry):
-                return one(xp, carry[0]), two(xp, carry[1])
-
-            return body
-
         blank = lambda n: jnp.zeros((n, nz), jnp.float32)
         fold = lambda v: jnp.sum(v, axis=0, keepdims=True)
 
@@ -606,16 +576,49 @@
         inside = inward(2, mover(2, ny - 2), blank(ny), 12)
         inward(3, damage, 0, 5)
 
-        low = open_stages(4, 8)
-        high = open_stages(4 - ny, 8)
-        unpack_y()
-        inward(1, pair(low[0], high[0]), (0, 0), 14)
-        unpack_y_clamp()
-        rims = inward(
-            2, pair(low[1](0, 2), high[1](ny - 2, ny)), (blank(8), blank(8)), 12
-        )
-        unpack_y_tough()
-        inward(3, pair(low[2], high[2]), (0, 0), 5)
+        if further > 1:
+            pl.semaphore_wait(r.reach.at[0], near_count)
+            greet(r.reach.at[1])
+
+        def rim(s):
+            above = (4, 4 - ny)[s]
+            stiffen, mover, damage = open_stages(above, 8)
+
+            def put_crack():
+                crack_pad[planes, y_out(s, 4)] = as_float(r.in_c[s])
+
+            def put_load():
+                for x in range(nx):
+                    held[HX + x, y_out(s, 5)] = as_float(r.in_l[s, 5 * x : 5 * x + 5])
+
+            def put_clamp():
+                for x in range(nx):
+                    clamped[HX + x, y_out(s, 3)] = as_float(r.in_f[s, 3 * x : 3 * x + 3])
+
+            def put_tough():
+                tough_pad[planes, y_out(s, 2)] = r.in_ty[s]
+
+            from_y(0, s, put_crack)
+            from_y(1, s, put_load)
+            inward(1, stiffen, 0, 14)
+            from_y(2, s, put_clamp)
+            counted = (0, 2) if s == 0 else (ny - 2, ny)
+            r.rims[s] = inward(2, mover(*counted), blank(8), 12)
+            from_y(3, s, put_tough)
+            inward(3, damage, 0, 10)
+
+        odd = lax.rem(gy, 2) == 1
+
+        @pl.when(odd)
+        def _():
+            rim(0)
+            rim(1)
+
+        @pl.when(jnp.logical_not(odd))
+        def _():
+            rim(1)
+            rim(0)
+
         stiffen1, mover1 = stages(1)
         move1 = mover1(OY, ny)
         inward(3, stiffen1, 0, 10)
@@ -626,7 +629,7 @@
         outward(2, 3, stiffen, 0)
         ends = outward(0, 2, mover(0, ny), blank(deep))
         outward(1, 1, mover(0, 0), blank(deep))
-        r.sums[me, 0:1] = fold(inside) + fold(rims[0] + rims[1]) + fold(ends)
+        r.sums[me, 0:1] = fold(inside) + fold(r.rims[0] + r.rims[1]) + fold(ends)
         outward(0, 3, damage, 0)
         outward(0, 3, stiffen1, 0)
         own = outward(-1, 3, move1, own)
@@ -648,7 +651,7 @@
         return own, finish
 
     def send_sums():
-        for k in range(further):
+        for k in range(1 if further > 1 else 0, further):
             pl.semaphore_wait(r.reach.at[k], near_count)
             if k + 1 < further:
                 greet(r.reach.at[k + 1])
@@ -979,6 +982,7 @@
         "in_k": vmem((4, 16, nz), jnp.int32),
         "in_kf": vmem((4, 4, nz), jnp.int32),
         "in_tk": vmem((4, 1, nz), f32),
+        "rims": vmem((2, 8, nz), f32),
         "sums": vmem((group, sections, nz), f32),
         "y_send": dma((8,)),
         "y_recv": dma((8,)),
@@ -988,7 +992,7 @@
         "b_recv": dma((16,)),
         "c_send": dma((8,)),
         "c_recv": dma((8,)),
-        "reach": pltpu.SemaphoreType.REGULAR((max(max(ngx, ngy) - 3, 1),)),
+        "reach": pltpu.SemaphoreType.REGULAR((max(max(ngx, ngy) - 2, 1),)),
         "tough_send": dma((later,)),
         "tough_recv": dma((later,)),
         "sum_send": dma((max(group - 1, 1),)),

time: 19 us -> 18.3 us (0.963)
  Pallas kernels: 17.6 us -> 16.8 us
    pallas_call x1, Pallas kernels: 16.3 us -> 15.5 us  [on_device(): pl.pallas_call(functools.partial(kernel, (sections, ngx, ngy, nx, ny, nz)...]
where the time goes in v8:
time: 18.3 us; the launch traced here: 18.1 us
  Pallas kernels  16.8 us (92%)
  between operations  1.28 us (7%)
    pallas_call x1, Pallas kernels, on_device(): pl.pallas_call(functools.partial(kernel, (sections, ngx, ngy, nx, ny, nz)...  15.5 us
    pallas_call x1, Pallas kernels, on_device(): pl.pallas_call(put_out, out_shape=(jax.ShapeDtypeStruct((1, 3, nx, ny, nz...  1.33 us

profile of v8, /device:TPU:0, one launch (start us, length us, event | category | flops | bytes accessed | tf_op | source)
XLA Modules:
  0.0 18.1 jit_solution(2596699548668000266)
XLA Ops:
  1.3 15.5 %shard_map.85 = (f32[16,16,128]{2,1,0:T(8,128)S(1)}, f32[16,16,128]{2,1,0:T(8,128)S(1)}, f32[16,16,128]{2,1,0:T(8,128)S(1)}, f32[16,16,128]{2,1,0:T(8,128)S(1)}, f32[1,2]{1,0:T(1,128)S(1)}) custom-call(s32[1]{0:T(128)S(6)} %copy.9.refs_0_, f32[3,64]{1,0:T(4,128)} %bitcast.1, f32[1,16,16,128]{3,2,1,0:T(8,128)} %refs_2_.1, s32[16,16,128]{2,1,0:T(8,128)} %refs_3_.1, ...), custom_call_target="tpu_custom_call" | custom-call | tf_op jit(solution)/shard_map/pallas_call | solution.py:1022
  16.8 1.3 %shard_map.86 = (f32[1,3,16,16,128]{4,3,2,1,0:T(8,128)}, f32[1,16,16,128]{3,2,1,0:T(8,128)}, f32[1,2]{1,0:T(1,128)}) custom-call(f32[16,16,128]{2,1,0:T(8,128)S(1)} %get-tuple-element.8.first_ref, f32[16,16,128]{2,1,0:T(8,128)S(1)} %get-tuple-element.9.second_ref, f32[16,16,128]{2,1,0:T(8,128)S(1)} %get-tuple-element.10.third_ref, ...), custom_call_target="tpu_custom_call" | custom-call | tf_op jit(solution)/shard_map/pallas_call | solution.py:1035

commit v9 on v8

--- a/solution.py
+++ b/solution.py
@@ -209,10 +209,12 @@
         crack_pad[xp] = zero
         clamped[xp] = zero + 1.0
         tough_pad[xp] = zero + 1.0
+        for f in range(3):
+            state[0, f, xp] = zero
         if sections > 2:
-            for p in range(2):
-                for f in range(4):
-                    state[p, f, xp] = zero
+            state[0, 3, xp] = zero
+            for f in range(4):
+                state[1, f, xp] = zero
         return carry
 
     lax.fori_loop(0, nx + 2 * HX, clear, 0)
@@ -222,22 +224,17 @@
 
     for s in range(2):
         side = lambda n, s=s: slice(0, n) if s == 0 else slice(ny - n, ny)
-        r.pack_c[s] = crack_ref[:, side(4)]
+        r.pack_l[s] = load_ref[:, side(4)]
+        r.pack_f[s] = clamp_ref[:, side(2)]
         for x in range(nx):
-            r.pack_l[s, 5 * x : 5 * x + 5] = load_ref[x, side(5)]
-            r.pack_f[s, 3 * x : 3 * x + 3] = clamp_ref[x, side(3)]
-    near_corner = (
-        (load_ref, held, 1, 4, 0),
-        (load_ref, held, 2, 3, 4),
-        (load_ref, held, 3, 2, 7),
-        (crack_ref, crack_pad, 1, 3, 9),
-        (crack_ref, crack_pad, 2, 2, 12),
-        (clamp_ref, clamped, 1, 2, 14),
-    )
-    far_corner = (
-        (load_ref, held, 4, 1, 0),
-        (crack_ref, crack_pad, 3, 1, 1),
-        (clamp_ref, clamped, 2, 1, 2),
+            r.pack_c[s, 3 * x : 3 * x + 3] = crack_ref[x, side(3)]
+    corner = (
+        (load_ref, held, 1, 3, 0),
+        (load_ref, held, 2, 2, 3),
+        (load_ref, held, 3, 1, 5),
+        (crack_ref, crack_pad, 1, 2, 6),
+        (crack_ref, crack_pad, 2, 1, 8),
+        (clamp_ref, clamped, 1, 1, 9),
     )
 
     def x_from(s, deep):
@@ -248,17 +245,15 @@
 
     for sx in range(2):
         for sy in range(2):
-            for pack, corner in ((r.pack_k, near_corner), (r.pack_kf, far_corner)):
-                for ref, _, deep, n, at in corner:
-                    first = 0 if sy == 0 else ny - n
-                    pack[sx * 2 + sy, at : at + n] = ref[x_from(sx, deep), first : first + n]
+            for ref, _, deep, n, at in corner:
+                first = 0 if sy == 0 else ny - n
+                r.pack_k[sx * 2 + sy, at : at + n] = ref[x_from(sx, deep), first : first + n]
 
     pl.semaphore_wait(barrier, near_count + sections - 1)
 
     beside_y = Exchange(r.y_send, r.y_recv)
     part_a = Exchange(r.a_send, r.a_recv)
     part_b = Exchange(r.b_send, r.b_recv)
-    part_c = Exchange(r.c_send, r.c_recv)
     for ex, ref, buf, deep, width, at, slot in (
         (part_a, load_ref, r.in_a, 3, 3, 0, 0),
         (part_a, crack_ref, r.in_a, 2, 2, 3, 2),
@@ -267,10 +262,6 @@
         (part_b, crack_ref, r.in_b, 3, 1, 1, 2),
         (part_b, clamp_ref, r.in_b, 2, 1, 2, 4),
         (part_b, tough_ref.at[0], r.in_tx, 1, 1, 0, 6),
-        (part_c, load_ref, r.in_c_x, 5, 1, 0, 0),
-        (part_c, crack_ref, r.in_c_x, 4, 1, 1, 2),
-        (part_c, clamp_ref, r.in_c_x, 3, 1, 2, 4),
-        (part_c, tough_ref.at[0], r.in_tx, 2, 1, 1, 6),
     ):
         for s in range(2):
             first = deep - width if s == 0 else nx - deep
@@ -296,29 +287,19 @@
     for sx in range(2):
         for sy in range(2):
             here, away = sx * 2 + sy, (1 - sx) * 2 + 1 - sy
-            for ex, pack, buf, slot in (
-                (part_a, r.pack_k, r.in_k, 6),
-                (part_b, r.pack_kf, r.in_kf, 8),
-                (part_b, r.pack_tk, r.in_tk, 12),
-            ):
-                ex.add(
-                    c_dev(sx, sy), pack.at[here], buf.at[away], buf.at[here],
-                    slot + away, slot + here,
-                )
+            part_a.add(
+                c_dev(sx, sy), r.pack_k.at[here], r.in_k.at[away], r.in_k.at[here],
+                6 + away, 6 + here,
+            )
     beside_y.start(0, 4)
     part_a.start(0, 6)
     beside_y.start(4, 6)
     fetch[3].wait()
     for s in range(2):
-        r.pack_t[s] = tough_ref[0, :, 0:2] if s == 0 else tough_ref[0, :, ny - 2 : ny]
-    for sx in range(2):
-        for sy in range(2):
-            row = 0 if sy == 0 else ny - 1
-            r.pack_tk[sx * 2 + sy] = tough_ref[0, 0 if sx == 0 else nx - 1, row : row + 1]
+        r.pack_t[s] = tough_ref[0, :, 0:1] if s == 0 else tough_ref[0, :, ny - 1 : ny]
     beside_y.start(6)
     part_a.start(6)
     part_b.start()
-    part_c.start()
     further = max(ngx, ngy) - 2
     if further > 0:
         greet(r.reach.at[0])
@@ -364,17 +345,6 @@
         beside_y.received(2 * kind + s, 2 * kind + s + 1)
         pl.when(there["gy"][s])(put)
 
-    def unpack_corners(corner, buf):
-        for sx in range(2):
-            for sy in range(2):
-
-                @pl.when(c_dev(sx, sy)[0])
-                def _(sx=sx, sy=sy):
-                    for _, pad, deep, n, at in corner:
-                        pad[x_at(sx, deep), y_out(sy, n)] = as_float(
-                            buf[sx * 2 + sy, at : at + n]
-                        )
-
     def unpack_a():
         part_a.received()
         for s in range(2):
@@ -385,31 +355,26 @@
                 crack_pad[x_out(s, 2), inner] = as_float(r.in_a[s, 3:5])
                 clamped[x_out(s, 1), inner] = as_float(r.in_a[s, 5:6])
 
-        unpack_corners(near_corner, r.in_k)
-
-    def unpack_far(part, buf, less):
-        part.received()
+        for sx in range(2):
+            for sy in range(2):
+
+                @pl.when(c_dev(sx, sy)[0])
+                def _(sx=sx, sy=sy):
+                    for _, pad, deep, n, at in corner:
+                        pad[x_at(sx, deep), y_out(sy, n)] = as_float(
+                            r.in_k[sx * 2 + sy, at : at + n]
+                        )
+
+    def unpack_b():
+        part_b.received()
         for s in range(2):
 
             @pl.when(there["gx"][s])
             def _(s=s):
-                held[x_at(s, 5 - less), inner] = as_float(buf[s, 0])
-                crack_pad[x_at(s, 4 - less), inner] = as_float(buf[s, 1])
-                clamped[x_at(s, 3 - less), inner] = as_float(buf[s, 2])
-                tough_pad[x_at(s, 2 - less), inner] = r.in_tx[s, 1 - less]
-
-    def unpack_b():
-        unpack_far(part_b, r.in_b, 1)
-        unpack_corners(far_corner, r.in_kf)
-        for sx in range(2):
-            for sy in range(2):
-
-                @pl.when(c_dev(sx, sy)[0])
-                def _(sx=sx, sy=sy):
-                    tough_pad[x_at(sx, 1), y_out(sy, 1)] = r.in_tk[sx * 2 + sy]
-
-    def unpack_c():
-        unpack_far(part_c, r.in_c_x, 0)
+                held[x_at(s, 4), inner] = as_float(r.in_b[s, 0])
+                crack_pad[x_at(s, 3), inner] = as_float(r.in_b[s, 1])
+                clamped[x_at(s, 2), inner] = as_float(r.in_b[s, 2])
+                tough_pad[x_at(s, 1), inner] = r.in_tx[s, 0]
 
     wide = up8(ny + 4)
     deep = up8(ny + 8)
@@ -585,18 +550,17 @@
             stiffen, mover, damage = open_stages(above, 8)
 
             def put_crack():
-                crack_pad[planes, y_out(s, 4)] = as_float(r.in_c[s])
+                for x in range(nx):
+                    crack_pad[HX + x, y_out(s, 3)] = as_float(r.in_c[s, 3 * x : 3 * x + 3])
 
             def put_load():
-                for x in range(nx):
-                    held[HX + x, y_out(s, 5)] = as_float(r.in_l[s, 5 * x : 5 * x + 5])
+                held[planes, y_out(s, 4)] = as_float(r.in_l[s])
 
             def put_clamp():
-                for x in range(nx):
-                    clamped[HX + x, y_out(s, 3)] = as_float(r.in_f[s, 3 * x : 3 * x + 3])
+                clamped[planes, y_out(s, 2)] = as_float(r.in_f[s])
 
             def put_tough():
-                tough_pad[planes, y_out(s, 2)] = r.in_ty[s]
+                tough_pad[planes, y_out(s, 1)] = r.in_ty[s]
 
             from_y(0, s, put_crack)
             from_y(1, s, put_load)
@@ -641,14 +605,7 @@
         outward(1, 1, stiffen1, 0)
         own = outward(0, 1, move1, own)
 
-        def finish():
-            unpack_c()
-            outward(4, 1, stiffen, 0)
-            outward(3, 1, mover(0, 0), blank(deep))
-            outward(2, 1, damage, 0)
-            outward(2, 1, stiffen1, 0)
-
-        return own, finish
+        return own
 
     def send_sums():
         for k in range(1 if further > 1 else 0, further):
@@ -725,22 +682,38 @@
         add_up(rnd, total)
         if done:
             send_sums()
-        if rnd == 1:
-            finish_open()
-        none = jnp.zeros((8, nz), jnp.float32)
-
-        def edges(xp, carry):
-            mover(OY - 4, 8)(xp, none)
-            mover(OY + ny - 3, 8)(xp, none)
-            return carry
-
-        lax.fori_loop(HX, HX + nx, edges, 0, unroll=part(nx, 8))
-        ends = mover(OY, ny)
-        ends(HX - 1, jnp.zeros((ny, nz), jnp.float32))
-        ends(HX + nx, jnp.zeros((ny, nz), jnp.float32))
         par = rnd % 2
         mid = pl.ds(OY, ny)
-        if not done:
+        if done:
+            rims = Exchange(r.v_send, r.v_recv)
+            for s in range(2):
+                row = OY if s == 0 else OY + ny - 1
+                for f in range(3):
+                    r.pack_v[s, f] = state[q, f, planes, row : row + 1]
+                rims.add(
+                    x_dev(s),
+                    state.at[q, pl.ds(0, 3), HX if s == 0 else HX + nx - 1, mid],
+                    r.in_vx.at[1 - s],
+                    r.in_vx.at[s],
+                    1 - s,
+                    s,
+                )
+                rims.add(
+                    y_dev(s), r.pack_v.at[s], r.in_vy.at[1 - s], r.in_vy.at[s], 3 - s, 2 + s
+                )
+            rims.start()
+            rims.received()
+            for s in range(2):
+
+                @pl.when(there["gx"][s])
+                def _(s=s):
+                    state[q, 0:3, x_at(s, 1), inner] = r.in_vx[s]
+
+                @pl.when(there["gy"][s])
+                def _(s=s):
+                    for f in range(3):
+                        state[q, f, planes, y_out(s, 1)] = r.in_vy[s, f]
+        else:
             for f in range(3):
                 r.pack_u[0, :, 2 * f : 2 * f + 2] = state[q, f, planes, OY : OY + 2]
                 r.pack_u[1, :, 2 * f : 2 * f + 2] = state[q, f, planes, OY + ny - 2 : OY + ny]
@@ -784,6 +757,31 @@
                         6 + sx * 2 + sy,
                     )
             shift.start()
+            shift.finish()
+            third_x = (HX - 3, HX + nx + 2)
+            third_y = (slice(OY - 3, OY - 2), slice(OY + ny + 2, OY + ny + 3))
+            for s in range(2):
+
+                @pl.when(there["gx"][s])
+                def _(s=s):
+                    state[q, 0:3, x_out(s, 2), inner] = r.in_u_x[par, s]
+                    state[q, 0, third_x[s], inner] = r.in_u_x3[par, s]
+
+                @pl.when(there["gy"][s])
+                def _(s=s):
+                    for f in range(3):
+                        state[q, f, planes, y_out(s, 2)] = r.in_u_y[par, s, :, 2 * f : 2 * f + 2]
+                    state[q, 1, planes, third_y[s]] = r.in_u_y[par, s, :, 6:7]
+
+            for sx in range(2):
+                for sy in range(2):
+
+                    @pl.when(c_dev(sx, sy)[0])
+                    def _(sx=sx, sy=sy):
+                        for f in range(3):
+                            state[q, f, x_out(sx, 2), y_out(sy, 2)] = r.in_u_c[
+                                par, sx * 2 + sy, :, 2 * f : 2 * f + 2
+                            ]
 
         tough_copies[rnd - 1].wait_recv()
 
@@ -810,6 +808,7 @@
 
         lax.fori_loop(0, nx, damage, 0, unroll=part(nx, 8))
         if done:
+            rims.sent()
             return
 
         r.pack_d[0] = state[q, 3, planes, OY : OY + 2]
@@ -844,32 +843,6 @@
                     4 + sx * 2 + sy,
                 )
         crack.start()
-        shift.finish()
-        third_x = (HX - 3, HX + nx + 2)
-        third_y = (slice(OY - 3, OY - 2), slice(OY + ny + 2, OY + ny + 3))
-        for s in range(2):
-
-            @pl.when(there["gx"][s])
-            def _(s=s):
-                state[q, 0:3, x_out(s, 2), inner] = r.in_u_x[par, s]
-                state[q, 0, third_x[s], inner] = r.in_u_x3[par, s]
-
-            @pl.when(there["gy"][s])
-            def _(s=s):
-                for f in range(3):
-                    state[q, f, planes, y_out(s, 2)] = r.in_u_y[par, s, :, 2 * f : 2 * f + 2]
-                state[q, 1, planes, third_y[s]] = r.in_u_y[par, s, :, 6:7]
-
-        for sx in range(2):
-            for sy in range(2):
-
-                @pl.when(c_dev(sx, sy)[0])
-                def _(sx=sx, sy=sy):
-                    for f in range(3):
-                        state[q, f, x_out(sx, 2), y_out(sy, 2)] = r.in_u_c[
-                            par, sx * 2 + sy, :, 2 * f : 2 * f + 2
-                        ]
-
         crack.finish()
         for s in range(2):
 
@@ -888,7 +861,7 @@
                 def _(sx=sx, sy=sy):
                     state[q, 3, x_out(sx, 1), y_out(sy, 2)] = r.in_d_c[par, sx * 2 + sy]
 
-    total, finish_open = open_sweep()
+    total = open_sweep()
     for rnd in range(1, sections):
         sweep(rnd, total)
 
@@ -896,7 +869,6 @@
     beside_y.sent()
     part_a.sent()
     part_b.sent()
-    part_c.sent()
     for copy in tough_copies:
         copy.wait_send()
     for k, peer in enumerate(peers):
@@ -964,34 +936,32 @@
         "tough_pad": vmem(padded, f32),
         "crack_pad": vmem(padded, f32),
         "tough_in": vmem((later, nx, ny, nz), f32),
-        "pack_l": vmem((2, 5 * nx, nz), jnp.int32),
-        "pack_f": vmem((2, 3 * nx, nz), jnp.int32),
-        "pack_c": vmem((2, nx, 4, nz), jnp.int32),
-        "pack_t": vmem((2, nx, 2, nz), f32),
+        "pack_l": vmem((2, nx, 4, nz), jnp.int32),
+        "pack_f": vmem((2, nx, 2, nz), jnp.int32),
+        "pack_c": vmem((2, 3 * nx, nz), jnp.int32),
+        "pack_t": vmem((2, nx, 1, nz), f32),
         "pack_k": vmem((4, 16, nz), jnp.int32),
-        "pack_kf": vmem((4, 4, nz), jnp.int32),
-        "pack_tk": vmem((4, 1, nz), f32),
         "in_a": vmem((2, 6, ny, nz), jnp.int32),
         "in_b": vmem((2, 3, ny, nz), jnp.int32),
-        "in_c_x": vmem((2, 3, ny, nz), jnp.int32),
-        "in_tx": vmem((2, 2, ny, nz), f32),
-        "in_l": vmem((2, 5 * nx, nz), jnp.int32),
-        "in_f": vmem((2, 3 * nx, nz), jnp.int32),
-        "in_c": vmem((2, nx, 4, nz), jnp.int32),
-        "in_ty": vmem((2, nx, 2, nz), f32),
+        "in_tx": vmem((2, 1, ny, nz), f32),
+        "in_l": vmem((2, nx, 4, nz), jnp.int32),
+        "in_f": vmem((2, nx, 2, nz), jnp.int32),
+        "in_c": vmem((2, 3 * nx, nz), jnp.int32),
+        "in_ty": vmem((2, nx, 1, nz), f32),
         "in_k": vmem((4, 16, nz), jnp.int32),
-        "in_kf": vmem((4, 4, nz), jnp.int32),
-        "in_tk": vmem((4, 1, nz), f32),
         "rims": vmem((2, 8, nz), f32),
+        "pack_v": vmem((2, 3, nx, 1, nz), f32),
+        "in_vx": vmem((2, 3, ny, nz), f32),
+        "in_vy": vmem((2, 3, nx, 1, nz), f32),
+        "v_send": dma((4,)),
+        "v_recv": dma((4,)),
         "sums": vmem((group, sections, nz), f32),
         "y_send": dma((8,)),
         "y_recv": dma((8,)),
         "a_send": dma((10,)),
         "a_recv": dma((10,)),
-        "b_send": dma((16,)),
-        "b_recv": dma((16,)),
-        "c_send": dma((8,)),
-        "c_recv": dma((8,)),
+        "b_send": dma((8,)),
+        "b_recv": dma((8,)),
         "reach": pltpu.SemaphoreType.REGULAR((max(max(ngx, ngy) - 2, 1),)),
         "tough_send": dma((later,)),
         "tough_recv": dma((later,)),

time: 18.3 us -> 17.9 us (0.978)
  Pallas kernels: 16.8 us -> 16.5 us
    pallas_call x1, Pallas kernels: 15.5 us -> 15.1 us  [on_device(): pl.pallas_call(functools.partial(kernel, (sections, ngx, ngy, nx, ny, nz)...]
where the time goes in v9:
time: 17.9 us; the launch traced here: 17.8 us
  Pallas kernels  16.5 us (92%)
  between operations  1.28 us (7%)
    pallas_call x1, Pallas kernels, on_device(): pl.pallas_call(functools.partial(kernel, (sections, ngx, ngy, nx, ny, nz)...  15.1 us
    pallas_call x1, Pallas kernels, on_device(): pl.pallas_call(put_out, out_shape=(jax.ShapeDtypeStruct((1, 3, nx, ny, nz...  1.33 us

profile of v9, /device:TPU:0, one launch (start us, length us, event | category | flops | bytes accessed | tf_op | source)
XLA Modules:
  0.0 17.8 jit_solution(4188769115931835044)
XLA Ops:
  1.3 15.1 %shard_map.85 = (f32[16,16,128]{2,1,0:T(8,128)S(1)}, f32[16,16,128]{2,1,0:T(8,128)S(1)}, f32[16,16,128]{2,1,0:T(8,128)S(1)}, f32[16,16,128]{2,1,0:T(8,128)S(1)}, f32[1,2]{1,0:T(1,128)S(1)}) custom-call(s32[1]{0:T(128)S(6)} %copy.9.refs_0_, f32[3,64]{1,0:T(4,128)} %bitcast.1, f32[1,16,16,128]{3,2,1,0:T(8,128)} %refs_2_.1, s32[16,16,128]{2,1,0:T(8,128)} %refs_3_.1, ...), custom_call_target="tpu_custom_call" | custom-call | tf_op jit(solution)/shard_map/pallas_call | solution.py:992
  16.4 1.3 %shard_map.86 = (f32[1,3,16,16,128]{4,3,2,1,0:T(8,128)}, f32[1,16,16,128]{3,2,1,0:T(8,128)}, f32[1,2]{1,0:T(1,128)}) custom-call(f32[16,16,128]{2,1,0:T(8,128)S(1)} %get-tuple-element.8.first_ref, f32[16,16,128]{2,1,0:T(8,128)S(1)} %get-tuple-element.9.second_ref, f32[16,16,128]{2,1,0:T(8,128)S(1)} %get-tuple-element.10.third_ref, ...), custom_call_target="tpu_custom_call" | custom-call | tf_op jit(solution)/shard_map/pallas_call | solution.py:1005

commit v10 on v9

--- a/solution.py
+++ b/solution.py
@@ -865,7 +865,6 @@
     for rnd in range(1, sections):
         sweep(rnd, total)
 
-    cells = 3.0 * nx * ngx * ny * ngy * nz
     beside_y.sent()
     part_a.sent()
     part_b.sent()
@@ -884,19 +883,23 @@
     total = r.sums[0]
     for k in range(1, group):
         total = total + r.sums[k]
-    entries = jnp.sqrt(jnp.sum(total, axis=1, keepdims=True) / cells)
-    column = lax.broadcasted_iota(jnp.int32, (1, sections), 1)
-    norms = jnp.zeros((1, sections), jnp.float32)
-    for rnd in range(sections):
-        norms = jnp.where(
-            column == lax.rem(sec + rnd, sections), entries[rnd : rnd + 1], norms
-        )
-    r.norm_ref[...] = norms
+    r.total_ref[...] = total
 
 
 def put_out(
-    first_ref, second_ref, third_ref, dam_ref, norm_ref, disp_hbm, dam_hbm, norm_out, sems
+    sizes,
+    first_ref,
+    second_ref,
+    third_ref,
+    dam_ref,
+    total_ref,
+    disp_hbm,
+    dam_hbm,
+    norm_hbm,
+    norm_ref,
+    sems,
 ):
+    sections, ngx, ngy, nx, ny, nz = sizes
     copies = [
         pltpu.make_async_copy(ref, disp_hbm.at[0, f], sems.at[f])
         for f, ref in enumerate((first_ref, second_ref, third_ref))
@@ -904,9 +907,21 @@
     copies.append(pltpu.make_async_copy(dam_ref, dam_hbm.at[0], sems.at[3]))
     for copy in copies:
         copy.start()
-    norm_out[...] = norm_ref[...]
+    sec = lax.axis_index("section")
+    cells = 3.0 * nx * ngx * ny * ngy * nz
+    entries = jnp.sqrt(jnp.sum(total_ref[...], axis=1, keepdims=True) / cells)
+    column = lax.broadcasted_iota(jnp.int32, (1, sections), 1)
+    norms = jnp.zeros((1, sections), jnp.float32)
+    for rnd in range(sections):
+        norms = jnp.where(
+            column == lax.rem(sec + rnd, sections), entries[rnd : rnd + 1], norms
+        )
+    norm_ref[...] = norms
+    last = pltpu.make_async_copy(norm_ref, norm_hbm, sems.at[4])
+    last.start()
     for copy in copies:
         copy.wait()
+    last.wait()
 
 
 def on_device(sizes, load_index, load_table, toughness, clamp_mask, load_mask, crack_mask):
@@ -985,7 +1000,7 @@
             "d_recv": dma((2, 8)),
         }
     ins = ("index_hbm", "table_hbm", "tough_hbm", "clamp_hbm", "load_hbm", "crack_hbm")
-    outs = ("first_ref", "second_ref", "third_ref", "dam_ref", "norm_ref")
+    outs = ("first_ref", "second_ref", "third_ref", "dam_ref", "total_ref")
     names = (*ins, *outs, *scratch)
     block = pl.BlockSpec(memory_space=pltpu.VMEM)
     away = pl.BlockSpec(memory_space=pltpu.HBM)
@@ -993,7 +1008,7 @@
         functools.partial(kernel, (sections, ngx, ngy, nx, ny, nz), names),
         out_shape=(
             *[jax.ShapeDtypeStruct((nx, ny, nz), f32)] * 4,
-            jax.ShapeDtypeStruct((1, sections), f32),
+            jax.ShapeDtypeStruct((sections, nz), f32),
         ),
         in_specs=[away] * 6,
         out_specs=(block,) * 5,
@@ -1003,15 +1018,15 @@
         ),
     )(load_index, pltpu.with_memory_space_constraint(load_table.T, pltpu.HBM), toughness, clamp_mask, load_mask, crack_mask)
     return pl.pallas_call(
-        put_out,
+        functools.partial(put_out, (sections, ngx, ngy, nx, ny, nz)),
         out_shape=(
             jax.ShapeDtypeStruct((1, 3, nx, ny, nz), f32),
             jax.ShapeDtypeStruct((1, nx, ny, nz), f32),
             jax.ShapeDtypeStruct((1, sections), f32),
         ),
         in_specs=[block] * 5,
-        out_specs=(away, away, block),
-        scratch_shapes=[dma((4,))],
+        out_specs=(away, away, away),
+        scratch_shapes=[vmem((1, sections), f32), dma((5,))],
         compiler_params=pltpu.CompilerParams(vmem_limit_bytes=1024 * 1024),
     )(*results)
 

time: 17.9 us -> 17.3 us (0.966)
  Pallas kernels: 16.5 us -> 15.9 us
    pallas_call x1, Pallas kernels: 1.33 us -> 0.83 us  [on_device(): pl.pallas_call(functools.partial(put_out, (sections, ngx, ngy, nx, ny, nz...]
where the time goes in v10:
time: 17.3 us; the launch traced here: 17.2 us
  Pallas kernels  15.9 us (92%)
  between operations  1.28 us (7%)
    pallas_call x1, Pallas kernels, on_device(): pl.pallas_call(functools.partial(kernel, (sections, ngx, ngy, nx, ny, nz)...  15.1 us
    pallas_call x1, Pallas kernels, on_device(): pl.pallas_call(functools.partial(put_out, (sections, ngx, ngy, nx, ny, nz...  0.83 us

profile of v10, /device:TPU:0, one launch (start us, length us, event | category | flops | bytes accessed | tf_op | source)
XLA Modules:
  0.0 17.2 jit_solution(2879307259291285789)
XLA Ops:
  1.3 15.1 %shard_map.85 = (f32[16,16,128]{2,1,0:T(8,128)S(1)}, f32[16,16,128]{2,1,0:T(8,128)S(1)}, f32[16,16,128]{2,1,0:T(8,128)S(1)}, f32[16,16,128]{2,1,0:T(8,128)S(1)}, f32[2,128]{1,0:T(2,128)S(1)}) custom-call(s32[1]{0:T(128)S(6)} %copy.9.refs_0_, f32[3,64]{1,0:T(4,128)} %bitcast.1, f32[1,16,16,128]{3,2,1,0:T(8,128)} %refs_2_.1, s32[16,16,128]{2,1,0:T(8,128)} %refs_3_.1, ...), custom_call_target="tpu_custom_call" | custom-call | tf_op jit(solution)/shard_map/pallas_call | solution.py:1007
  16.3 0.8 %shard_map.86 = (f32[1,3,16,16,128]{4,3,2,1,0:T(8,128)}, f32[1,16,16,128]{3,2,1,0:T(8,128)}, f32[1,2]{1,0:T(1,128)}) custom-call(f32[16,16,128]{2,1,0:T(8,128)S(1)} %get-tuple-element.8.first_ref, f32[16,16,128]{2,1,0:T(8,128)S(1)} %get-tuple-element.9.second_ref, f32[16,16,128]{2,1,0:T(8,128)S(1)} %get-tuple-element.10.third_ref, ...), custom_call_target="tpu_custom_call" | custom-call | tf_op jit(solution)/shard_map/pallas_call | solution.py:1020

commit v11 on v10

--- a/solution.py
+++ b/solution.py
@@ -253,11 +253,14 @@
 
     beside_y = Exchange(r.y_send, r.y_recv)
     part_a = Exchange(r.a_send, r.a_recv)
+    part_m = Exchange(r.m_send, r.m_recv)
     part_b = Exchange(r.b_send, r.b_recv)
     for ex, ref, buf, deep, width, at, slot in (
-        (part_a, load_ref, r.in_a, 3, 3, 0, 0),
-        (part_a, crack_ref, r.in_a, 2, 2, 3, 2),
-        (part_a, clamp_ref, r.in_a, 1, 1, 5, 4),
+        (part_a, load_ref, r.in_a, 2, 2, 0, 0),
+        (part_a, crack_ref, r.in_a, 1, 1, 2, 2),
+        (part_m, load_ref, r.in_m, 3, 1, 0, 0),
+        (part_m, crack_ref, r.in_m, 2, 1, 1, 2),
+        (part_m, clamp_ref, r.in_m, 1, 1, 2, 4),
         (part_b, load_ref, r.in_b, 4, 1, 0, 0),
         (part_b, crack_ref, r.in_b, 3, 1, 1, 2),
         (part_b, clamp_ref, r.in_b, 2, 1, 2, 4),
@@ -289,16 +292,17 @@
             here, away = sx * 2 + sy, (1 - sx) * 2 + 1 - sy
             part_a.add(
                 c_dev(sx, sy), r.pack_k.at[here], r.in_k.at[away], r.in_k.at[here],
-                6 + away, 6 + here,
+                4 + away, 4 + here,
             )
     beside_y.start(0, 4)
-    part_a.start(0, 6)
+    part_a.start(0, 4)
     beside_y.start(4, 6)
     fetch[3].wait()
     for s in range(2):
         r.pack_t[s] = tough_ref[0, :, 0:1] if s == 0 else tough_ref[0, :, ny - 1 : ny]
     beside_y.start(6)
-    part_a.start(6)
+    part_a.start(4)
+    part_m.start()
     part_b.start()
     further = max(ngx, ngy) - 2
     if further > 0:
@@ -351,9 +355,8 @@
 
             @pl.when(there["gx"][s])
             def _(s=s):
-                held[x_out(s, 3), inner] = as_float(r.in_a[s, 0:3])
-                crack_pad[x_out(s, 2), inner] = as_float(r.in_a[s, 3:5])
-                clamped[x_out(s, 1), inner] = as_float(r.in_a[s, 5:6])
+                held[x_out(s, 2), inner] = as_float(r.in_a[s, 0:2])
+                crack_pad[x_out(s, 1), inner] = as_float(r.in_a[s, 2:3])
 
         for sx in range(2):
             for sy in range(2):
@@ -364,6 +367,16 @@
                         pad[x_at(sx, deep), y_out(sy, n)] = as_float(
                             r.in_k[sx * 2 + sy, at : at + n]
                         )
+
+    def unpack_m():
+        part_m.received()
+        for s in range(2):
+
+            @pl.when(there["gx"][s])
+            def _(s=s):
+                held[x_at(s, 3), inner] = as_float(r.in_m[s, 0])
+                crack_pad[x_at(s, 2), inner] = as_float(r.in_m[s, 1])
+                clamped[x_at(s, 1), inner] = as_float(r.in_m[s, 2])
 
     def unpack_b():
         part_b.received()
@@ -590,13 +603,19 @@
 
         stiffen, mover, damage = open_stages(4, deep)
         unpack_a()
-        outward(2, 3, stiffen, 0)
+        outward(1, 2, stiffen, 0)
         ends = outward(0, 2, mover(0, ny), blank(deep))
+        r.sums[me, 0:1] = fold(inside) + fold(r.rims[0] + r.rims[1]) + fold(ends)
+        outward(-1, 2, damage, 0)
+        outward(-1, 2, stiffen1, 0)
+        own = outward(-2, 2, move1, own)
+
+        unpack_m()
+        outward(2, 1, stiffen, 0)
         outward(1, 1, mover(0, 0), blank(deep))
-        r.sums[me, 0:1] = fold(inside) + fold(r.rims[0] + r.rims[1]) + fold(ends)
-        outward(0, 3, damage, 0)
-        outward(0, 3, stiffen1, 0)
-        own = outward(-1, 3, move1, own)
+        outward(0, 1, damage, 0)
+        outward(0, 1, stiffen1, 0)
+        own = outward(-1, 1, move1, own)
 
         unpack_b()
         outward(3, 1, stiffen, 0)
@@ -867,6 +886,7 @@
 
     beside_y.sent()
     part_a.sent()
+    part_m.sent()
     part_b.sent()
     for copy in tough_copies:
         copy.wait_send()
@@ -956,7 +976,8 @@
         "pack_c": vmem((2, 3 * nx, nz), jnp.int32),
         "pack_t": vmem((2, nx, 1, nz), f32),
         "pack_k": vmem((4, 16, nz), jnp.int32),
-        "in_a": vmem((2, 6, ny, nz), jnp.int32),
+        "in_a": vmem((2, 3, ny, nz), jnp.int32),
+        "in_m": vmem((2, 3, ny, nz), jnp.int32),
         "in_b": vmem((2, 3, ny, nz), jnp.int32),
         "in_tx": vmem((2, 1, ny, nz), f32),
         "in_l": vmem((2, nx, 4, nz), jnp.int32),
@@ -973,8 +994,10 @@
         "sums": vmem((group, sections, nz), f32),
         "y_send": dma((8,)),
         "y_recv": dma((8,)),
-        "a_send": dma((10,)),
-        "a_recv": dma((10,)),
+        "a_send": dma((8,)),
+        "a_recv": dma((8,)),
+        "m_send": dma((6,)),
+        "m_recv": dma((6,)),
         "b_send": dma((8,)),
         "b_recv": dma((8,)),
         "reach": pltpu.SemaphoreType.REGULAR((max(max(ngx, ngy) - 2, 1),)),

time: 17.3 us -> 17.2 us (level)
  no operation moved by 1% of the time
where the time goes in v11:
time: 17.2 us; the launch traced here: 17.1 us
  Pallas kernels  15.8 us (92%)
  between operations  1.28 us (7%)
    pallas_call x1, Pallas kernels, on_device(): pl.pallas_call(functools.partial(kernel, (sections, ngx, ngy, nx, ny, nz)...  15 us
    pallas_call x1, Pallas kernels, on_device(): pl.pallas_call(functools.partial(put_out, (sections, ngx, ngy, nx, ny, nz...  0.83 us

profile of v11, /device:TPU:0, one launch (start us, length us, event | category | flops | bytes accessed | tf_op | source)
XLA Modules:
  0.0 17.1 jit_solution(7040789948143470929)
XLA Ops:
  1.3 15.0 %shard_map.85 = (f32[16,16,128]{2,1,0:T(8,128)S(1)}, f32[16,16,128]{2,1,0:T(8,128)S(1)}, f32[16,16,128]{2,1,0:T(8,128)S(1)}, f32[16,16,128]{2,1,0:T(8,128)S(1)}, f32[2,128]{1,0:T(2,128)S(1)}) custom-call(s32[1]{0:T(128)S(6)} %copy.9.refs_0_, f32[3,64]{1,0:T(4,128)} %bitcast.1, f32[1,16,16,128]{3,2,1,0:T(8,128)} %refs_2_.1, s32[16,16,128]{2,1,0:T(8,128)} %refs_3_.1, ...), custom_call_target="tpu_custom_call" | custom-call | tf_op jit(solution)/shard_map/pallas_call | solution.py:1030
  16.2 0.8 %shard_map.86 = (f32[1,3,16,16,128]{4,3,2,1,0:T(8,128)}, f32[1,16,16,128]{3,2,1,0:T(8,128)}, f32[1,2]{1,0:T(1,128)}) custom-call(f32[16,16,128]{2,1,0:T(8,128)S(1)} %get-tuple-element.8.first_ref, f32[16,16,128]{2,1,0:T(8,128)S(1)} %get-tuple-element.9.second_ref, f32[16,16,128]{2,1,0:T(8,128)S(1)} %get-tuple-element.10.third_ref, ...), custom_call_target="tpu_custom_call" | custom-call | tf_op jit(solution)/shard_map/pallas_call | solution.py:1043

commit v12 on v11

--- a/solution.py
+++ b/solution.py
@@ -47,13 +47,13 @@
     dx = xx - mid
     dy = yy - mid
     dz = zz - mid
-    xy2 = xy * xy
-    xz2 = xz * xz
-    yz2 = yz * yz
+    xy2 = 0.25 * (xy * xy)
+    xz2 = 0.25 * (xz * xz)
+    yz2 = 0.25 * (yz * yz)
     sixth = (dx * dx + dy * dy + dz * dz + 2.0 * (xy2 + xz2 + yz2)) * (1.0 / 6.0)
     twice_radius = 2.0 * root(sixth)
-    scale = lax.rsqrt(sixth + eigen_guard)
-    det = dx * (dy * dz - yz2) - dz * xy2 - dy * xz2 + 2.0 * (xy * xz * yz)
+    scale = lax.rsqrt(sixth + 4.0 * eigen_guard)
+    det = dx * (dy * dz - yz2) - dz * xy2 - dy * xz2 + 0.25 * (xy * xz * yz)
     ratio = (0.5 * det * scale) * (scale * scale)
     size = jnp.minimum(jnp.abs(ratio), 1.0)
     poly = jnp.full_like(size, ACOS[-1] / 3.0)
@@ -454,13 +454,13 @@
                 )
             )
             keep(f, here)
-        return 2.0 * spectral_energy(
-            0.5 * grad[0][0],
-            0.5 * grad[1][1],
-            0.5 * grad[2][2],
-            0.25 * (grad[0][1] + grad[1][0]),
-            0.25 * (grad[0][2] + grad[2][0]),
-            0.25 * (grad[1][2] + grad[2][1]),
+        return 0.5 * spectral_energy(
+            grad[0][0],
+            grad[1][1],
+            grad[2][2],
+            grad[0][1] + grad[1][0],
+            grad[0][2] + grad[2][0],
+            grad[1][2] + grad[2][1],
         )
 
     def renew(at, d, energy, g, cracked, first, last):
@@ -554,10 +554,6 @@
         inside = inward(2, mover(2, ny - 2), blank(ny), 12)
         inward(3, damage, 0, 5)
 
-        if further > 1:
-            pl.semaphore_wait(r.reach.at[0], near_count)
-            greet(r.reach.at[1])
-
         def rim(s):
             above = (4, 4 - ny)[s]
             stiffen, mover, damage = open_stages(above, 8)
@@ -595,6 +591,10 @@
         def _():
             rim(1)
             rim(0)
+
+        if further > 1:
+            pl.semaphore_wait(r.reach.at[0], near_count)
+            greet(r.reach.at[1])
 
         stiffen1, mover1 = stages(1)
         move1 = mover1(OY, ny)

time: 17.2 us -> 17.3 us (level)
  no operation moved by 1% of the time
where the time goes in v12:
time: 17.3 us; the launch traced here: 17.2 us
  Pallas kernels  15.9 us (92%)
  between operations  1.28 us (7%)
    pallas_call x1, Pallas kernels, on_device(): pl.pallas_call(functools.partial(kernel, (sections, ngx, ngy, nx, ny, nz)...  15.1 us
    pallas_call x1, Pallas kernels, on_device(): pl.pallas_call(functools.partial(put_out, (sections, ngx, ngy, nx, ny, nz...  0.83 us

profile of v12, /device:TPU:0, one launch (start us, length us, event | category | flops | bytes accessed | tf_op | source)
XLA Modules:
  0.0 17.2 jit_solution(10307095334010056377)
XLA Ops:
  1.3 15.1 %shard_map.85 = (f32[16,16,128]{2,1,0:T(8,128)S(1)}, f32[16,16,128]{2,1,0:T(8,128)S(1)}, f32[16,16,128]{2,1,0:T(8,128)S(1)}, f32[16,16,128]{2,1,0:T(8,128)S(1)}, f32[2,128]{1,0:T(2,128)S(1)}) custom-call(s32[1]{0:T(128)S(6)} %copy.9.refs_0_, f32[3,64]{1,0:T(4,128)} %bitcast.1, f32[1,16,16,128]{3,2,1,0:T(8,128)} %refs_2_.1, s32[16,16,128]{2,1,0:T(8,128)} %refs_3_.1, ...), custom_call_target="tpu_custom_call" | custom-call | tf_op jit(solution)/shard_map/pallas_call | solution.py:1030
  16.3 0.8 %shard_map.86 = (f32[1,3,16,16,128]{4,3,2,1,0:T(8,128)}, f32[1,16,16,128]{3,2,1,0:T(8,128)}, f32[1,2]{1,0:T(1,128)}) custom-call(f32[16,16,128]{2,1,0:T(8,128)S(1)} %get-tuple-element.8.first_ref, f32[16,16,128]{2,1,0:T(8,128)S(1)} %get-tuple-element.9.second_ref, f32[16,16,128]{2,1,0:T(8,128)S(1)} %get-tuple-element.10.third_ref, ...), custom_call_target="tpu_custom_call" | custom-call | tf_op jit(solution)/shard_map/pallas_call | solution.py:1043

commit v13 on v11

--- a/solution.py
+++ b/solution.py
@@ -129,7 +129,6 @@
                 pl.semaphore_signal(sem, inc=1, device_id=dev, device_id_type=MESH)
 
     barrier = pltpu.get_barrier_semaphore()
-    greet(barrier)
     for k in range(1, sections):
         pl.semaphore_signal(
             barrier,
@@ -137,6 +136,7 @@
             device_id={"section": lax.rem(sec + k, sections)},
             device_id_type=MESH,
         )
+    greet(barrier)
 
     fetch = [
         pltpu.make_async_copy(src, dst, local.at[n])

time: 17.2 us -> 17.2 us (level)
  no operation moved by 1% of the time
where the time goes in v13:
time: 17.2 us; the launch traced here: 17.1 us
  Pallas kernels  15.8 us (92%)
  between operations  1.28 us (7%)
    pallas_call x1, Pallas kernels, on_device(): pl.pallas_call(functools.partial(kernel, (sections, ngx, ngy, nx, ny, nz)...  15 us
    pallas_call x1, Pallas kernels, on_device(): pl.pallas_call(functools.partial(put_out, (sections, ngx, ngy, nx, ny, nz...  0.83 us

profile of v13, /device:TPU:0, one launch (start us, length us, event | category | flops | bytes accessed | tf_op | source)
XLA Modules:
  0.0 17.1 jit_solution(3022240902224146530)
XLA Ops:
  1.3 15.0 %shard_map.85 = (f32[16,16,128]{2,1,0:T(8,128)S(1)}, f32[16,16,128]{2,1,0:T(8,128)S(1)}, f32[16,16,128]{2,1,0:T(8,128)S(1)}, f32[16,16,128]{2,1,0:T(8,128)S(1)}, f32[2,128]{1,0:T(2,128)S(1)}) custom-call(s32[1]{0:T(128)S(6)} %copy.9.refs_0_, f32[3,64]{1,0:T(4,128)} %bitcast.1, f32[1,16,16,128]{3,2,1,0:T(8,128)} %refs_2_.1, s32[16,16,128]{2,1,0:T(8,128)} %refs_3_.1, ...), custom_call_target="tpu_custom_call" | custom-call | tf_op jit(solution)/shard_map/pallas_call | solution.py:1030
  16.3 0.8 %shard_map.86 = (f32[1,3,16,16,128]{4,3,2,1,0:T(8,128)}, f32[1,16,16,128]{3,2,1,0:T(8,128)}, f32[1,2]{1,0:T(1,128)}) custom-call(f32[16,16,128]{2,1,0:T(8,128)S(1)} %get-tuple-element.8.first_ref, f32[16,16,128]{2,1,0:T(8,128)S(1)} %get-tuple-element.9.second_ref, f32[16,16,128]{2,1,0:T(8,128)S(1)} %get-tuple-element.10.third_ref, ...), custom_call_target="tpu_custom_call" | custom-call | tf_op jit(solution)/shard_map/pallas_call | solution.py:1043
